TPU v7x, 512 devices: a whole 4x8x8 slice. The times are simulated.
512 devices in a mesh: fluid: 64 (over z, x, core), solid: 8 (over y).
Axes of the slice: x: 4, y: 8, z: 8, core: 2. Of those that a mesh axis runs over, the one named last changes fastest.
Arguments:
- fluid_load: float32 [32768, 3, 128], P(('fluid', 'solid')), may hold values from -6 to 6
- stiffness: float32 [32768, 3, 128], P(('fluid', 'solid')), may hold values from 0.2 to 2
- mapping: bfloat16 [32768, 128, 128], P(('fluid', 'solid')), may hold values from -0.5 to 0.5
- live_count: int32 [512], P(('fluid', 'solid')), may hold values from 40 to 64, as said below
- dest_device: int32 [32768, 1], P(('fluid', 'solid')), may hold values from 0 to 63; in each aligned block of 64 rows (0 to 63, 64 to 127, ...) at most 2 rows name the same one
- local_block: int32 [32768], P(('fluid', 'solid')), may hold values from 0 to 3
- compliance: float32 [8, 256, 3, 128], P('solid', 'fluid'), may hold values from 0.05 to 0.5
- start_disp: float32 [8, 256, 3, 128], P('solid', 'fluid'), may hold values from -40 to 40
- residual_history: float32 [50, 8, 256, 3, 128], P(None, 'solid', 'fluid'), may hold values from -40 to 40
- update_history: float32 [50, 8, 256, 3, 128], P(None, 'solid', 'fluid'), may hold values from -2.4 to 2.4
Outputs:
- displacement: float32 [8, 256, 3, 128], P('solid', 'fluid')
- fluid_displacement: float32 [32768, 3, 128], P(('fluid', 'solid'))
Inputs may be any that keep to these rules, and one draw needn't show every extreme that they name: `live_count`: each device's live blocks are its first ones; some device has exactly 64. `dest_device`: among the 64 rows of one device no fluid index appears more than 2 times.
All inputs are finite; a program needn't handle non-finite values.
Results may differ from a plain program's by a relative error of at most 0.0094.
Values may be sent and summed in bfloat16 or wider, within the bound.
No kernel may reach another device: no remote copies, remote signals or barrier semaphores. Data moves between devices by JAX's collectives and lax.ppermute only.
A program may use at most 64 MiB of HBM per device.

v0:
```python
import jax
import jax.numpy as jnp
from jax import lax
from jax.sharding import Mesh
from jax.sharding import PartitionSpec as P

ITERS = 2
FLUID_SOLID = ("fluid_0", "fluid_1", "fluid_2", "solid")
FLUID = ("fluid_0", "fluid_1", "fluid_2")


ridge_share = 0.01


def over_axes(x, axes):
    for axis in axes:
        x = lax.psum(x, axis)
    return x


def sent_to_all(x, axis):
    copies = jnp.broadcast_to(x, (lax.axis_size(axis), *x.shape))
    return lax.all_to_all(copies, axis, split_axis=0, concat_axis=0, tiled=True)


def in_order(parts, dim):
    dims = list(parts.shape[1:])
    dims[dim] *= parts.shape[0]
    return jnp.moveaxis(parts, 0, dim).reshape(dims)


def gathered_copies(x, axis, dim):
    parts = sent_to_all(x, axis)
    return in_order(parts, dim)


def in_blocks(x, dim, count):
    before, after = (x.shape[:dim], x.shape[dim + 1 :])
    return jnp.moveaxis(x.reshape(*before, count, -1, *after), dim, 0)


def sum_at_owner(x, axis, dim):
    count = lax.axis_size(axis)
    parts = lax.all_to_all(in_blocks(x, dim, count), axis, 0, 0, tiled=True)
    return jnp.sum(parts.astype(jnp.float32), axis=0)


def solve_small(gram_matrix, right_side):
    order = gram_matrix.shape[0]
    ridge = ridge_share * jnp.trace(gram_matrix) / order
    factor = jnp.linalg.cholesky(gram_matrix + ridge * jnp.eye(order, dtype=gram_matrix.dtype))
    halfway = lax.linalg.triangular_solve(factor, right_side[:, None], left_side=True, lower=True)
    solved = lax.linalg.triangular_solve(
        factor, halfway, left_side=True, lower=True, transpose_a=True
    )
    return -solved[:, 0]


def full_sums(basis_flat, resid_flat):
    gram_local = jnp.dot(basis_flat, basis_flat.T, precision=lax.Precision.HIGHEST)
    right_local = jnp.dot(basis_flat, resid_flat, precision=lax.Precision.HIGHEST)
    return (over_axes(gram_local, FLUID_SOLID), over_axes(right_local, FLUID_SOLID))


def body(
    fluid_load,
    stiffness,
    mapping,
    live_count,
    dest_device,
    local_block,
    compliance,
    start_disp,
    residual_history,
    update_history,
):
    blocks = mapping.shape[0]
    sub_blocks = compliance.shape[1]
    alive = (jnp.arange(blocks) < live_count[0]).astype(jnp.float32)[:, None, None]
    target = dest_device[:, 0] * sub_blocks + local_block

    def to_fluid(struct_disp):
        packed = struct_disp[0].astype(jnp.bfloat16)
        pieces = gathered_copies(packed, FLUID, 0)
        onehot = (target[:, None] == jnp.arange(pieces.shape[0])[None, :]).astype(jnp.bfloat16)
        picked = jnp.einsum("bk,kcj->bcj", onehot, pieces, preferred_element_type=jnp.float32)
        fluid_disp = jnp.einsum(
            "bjn,bcj->bcn", mapping, picked.astype(jnp.bfloat16), preferred_element_type=jnp.float32
        )
        return fluid_disp * alive

    struct_disp = start_disp
    basis_cols = residual_history
    updates = update_history
    last_resid = struct_disp
    last_image = struct_disp
    gram_matrix = None
    for iteration in range(ITERS):
        fluid_disp = to_fluid(struct_disp)
        fluid_force = (alive * (fluid_load - stiffness * fluid_disp)).astype(jnp.bfloat16)
        contrib = jnp.einsum(
            "bjn,bcn->bcj", mapping, fluid_force, preferred_element_type=jnp.float32
        )
        force_onehot = (
            jnp.arange(sub_blocks * lax.axis_size(FLUID))[:, None] == target[None, :]
        ).astype(jnp.float32)
        summed = sum_at_owner(
            jnp.einsum(
                "rb,bcj->rcj", force_onehot, contrib, precision=lax.Precision.HIGHEST
            ).astype(jnp.bfloat16),
            FLUID,
            0,
        )
        struct_image = compliance * summed[None]
        residual = struct_image - struct_disp
        newest = residual - last_resid
        if iteration > 0:
            basis_cols = jnp.concatenate([basis_cols[1:], newest[None]], 0)
            updates = jnp.concatenate([updates[1:], (struct_image - last_image)[None]], 0)
        basis_flat = basis_cols.reshape(basis_cols.shape[0], -1)
        resid_flat = residual.reshape(-1)
        if iteration == 0:
            gram_matrix, right_side = full_sums(basis_flat, resid_flat)
        else:
            row_local = jnp.dot(basis_flat, newest.reshape(-1), precision=lax.Precision.HIGHEST)
            right_local = jnp.dot(basis_flat, resid_flat, precision=lax.Precision.HIGHEST)
            new_row, right_side = (
                over_axes(row_local, FLUID_SOLID),
                over_axes(right_local, FLUID_SOLID),
            )
            upper_part = jnp.concatenate([gram_matrix[1:, 1:], new_row[:-1, None]], 1)
            gram_matrix = jnp.concatenate([upper_part, new_row[None, :]], 0)
        coefficients = solve_small(gram_matrix, right_side)
        struct_disp = struct_image + jnp.tensordot(
            coefficients, updates, axes=1, precision=lax.Precision.HIGHEST
        )
        last_resid = residual
        last_image = struct_image
    final_disp = to_fluid(struct_disp)
    return (struct_disp, final_disp)


def solution(mesh):
    split = Mesh(
        mesh.devices.reshape(8, 4, 2, mesh.shape["solid"]),
        ("fluid_0", "fluid_1", "fluid_2", "solid"),
    )
    in_specs = (
        P(FLUID_SOLID, None, None),
        P(FLUID_SOLID, None, None),
        P(FLUID_SOLID, None, None),
        P(FLUID_SOLID),
        P(FLUID_SOLID, None),
        P(FLUID_SOLID),
        P("solid", FLUID, None, None),
        P("solid", FLUID, None, None),
        P(None, "solid", FLUID, None, None),
        P(None, "solid", FLUID, None, None),
    )
    out_specs = (P("solid", FLUID, None, None), P(FLUID_SOLID, None, None))
    return jax.shard_map(body, mesh=split, in_specs=in_specs, out_specs=out_specs, check_vma=False)
```

profile of v0, /device:TPU:1, one launch (start us, length us, event | category | flops | bytes accessed | tf_op | source)
XLA Modules:
  0.0 251.1 jit_solution(15389651478953611320)
XLA Ops:
  0.6 0.8 convert_bitcast_fusion.2
  1.5 0.7 broadcast_in_dim.50
  2.2 14.8 %all-to-all-start = ((bf16[64,4,3,128]{3,1,2,0:T(4,128)(2,1)}), bf16[64,4,3,128]{3,1,2,0:T(4,128)(2,1)S(1)}, u32[]{:S(2)}, u32[]{:S(2)}) async-start(bf16[64,4,3,128]{3,1,2,0:T(4,128)(2,1)} %broadcast_in_dim.50), calls=%async_computation | async-start | bytes 393216 | tf_op jit(solution)/shard_map/all_to_all | solution.py:23
  17.7 0.7 bitcast_add_fusion.2
  18.4 10.7 %all-to-all-done = bf16[64,4,3,128]{3,1,2,0:T(4,128)(2,1)S(1)} async-done(((bf16[64,4,3,128]{3,1,2,0:T(4,128)(2,1)}), bf16[64,4,3,128]{3,1,2,0:T(4,128)(2,1)S(1)}, u32[]{:S(2)}, u32[]{:S(2)}) %all-to-all-start) | async-done | bytes 196640 | tf_op jit(solution)/shard_map/all_to_all | solution.py:23
  29.4 2.7 %fusion.9 = f32[64,3,128]{2,1,0:T(4,128)S(1)} fusion(bf16[64,128,128]{2,1,0:T(8,128)(2,1)S(1)} %copy-done, f32[64,3,128]{2,0,1:T(8,128)} %param.15, f32[64,3,128]{2,0,1:T(8,128)} %param.16, bf16[64,3,128]{2,0,1:T(8,128)(2,1)S(1)} %convolution_convert_fusion.4, f32[64]{0:T(128)S(1)} %compare_convert_fusion), kind=kOutput, calls=%fused_computation.17 | convolution fusion | flops 12705792 | bytes 2441472 | tf_op jit(solution)/shard_map/bjn,bcn->bcj/dot_general | solution.py:101
  32.5 0.7 copy.44
  33.3 4.5 %all-to-all-start.1 = ((bf16[64,4,3,128]{3,1,2,0:T(4,128)(2,1)}), bf16[64,4,3,128]{3,1,2,0:T(4,128)(2,1)S(1)}, u32[]{:S(2)}, u32[]{:S(2)}) async-start(bf16[64,4,3,128]{3,1,2,0:T(4,128)(2,1)} %copy.44), calls=%async_computation.1 | async-start | bytes 393216 | tf_op jit(solution)/shard_map/all_to_all | solution.py:44
  38.2 11.7 %all-to-all-done.1 = bf16[64,4,3,128]{3,1,2,0:T(4,128)(2,1)S(1)} async-done(((bf16[64,4,3,128]{3,1,2,0:T(4,128)(2,1)}), bf16[64,4,3,128]{3,1,2,0:T(4,128)(2,1)S(1)}, u32[]{:S(2)}, u32[]{:S(2)}) %all-to-all-start.1) | async-done | bytes 196640 | tf_op jit(solution)/shard_map/all_to_all | solution.py:44
  50.4 21.0 %all-reduce.3 = (f32[50]{0:T(128)S(1)}, f32[50,50]{0,1:T(8,128)S(1)}) all-reduce(f32[50]{0:T(128)S(1)} %convolution_bitcast_fusion.3, f32[50,50]{0,1:T(8,128)S(1)} %convolution_bitcast_fusion), channel_id=1, replica_groups=mesh['fluid_0'=8,'fluid_1'=4,'fluid_2'=2,'solid'=8] {'fluid_0'}, use_global_device_ids=true, to_apply=%region_8.10 | all-reduce | flops 2550 | bytes 20400 | tf_op jit(solution)/shard_map/psum | solution.py:17
  71.4 11.7 %all-reduce.5 = (f32[50]{0:T(128)S(1)}, f32[50,50]{0,1:T(8,128)S(1)}) all-reduce(f32[50]{0:T(128)S(1)} %get-tuple-element.17, f32[50,50]{0,1:T(8,128)S(1)} %get-tuple-element.18), channel_id=1, replica_groups=mesh['fluid_0'=8,'fluid_1'=4,'fluid_2'=2,'solid'=8] {'fluid_1'}, use_global_device_ids=true, to_apply=%region_9.0 | all-reduce | flops 2550 | bytes 20400 | tf_op jit(solution)/shard_map/psum | solution.py:17
  83.1 14.6 %all-reduce.7 = (f32[50]{0:T(128)S(1)}, f32[50,50]{0,1:T(8,128)S(1)}) all-reduce(f32[50]{0:T(128)S(1)} %get-tuple-element.21, f32[50,50]{0,1:T(8,128)S(1)} %get-tuple-element.22), channel_id=1, replica_groups=mesh['fluid_0'=8,'fluid_1'=4,'fluid_2'=2,'solid'=8] {'fluid_2'}, use_global_device_ids=true, to_apply=%region_10.12 | all-reduce | flops 2550 | bytes 20400 | tf_op jit(solution)/shard_map/psum | solution.py:17
  97.7 23.2 %all-reduce.1 = (f32[50,1]{0,1:T(1,128)S(1)}, f32[50,50]{0,1:T(8,128)S(1)}) all-reduce(f32[50,1]{0,1:T(1,128)S(1)} %bitcast.163, f32[50,50]{0,1:T(8,128)S(1)} %get-tuple-element.26), channel_id=1, replica_groups=mesh['fluid_0'=8,'fluid_1'=4,'fluid_2'=2,'solid'=8] {'solid'}, use_global_device_ids=true, to_apply=%region_11.13 | all-reduce | flops 2550 | bytes 20400 | tf_op jit(solution)/shard_map/psum | solution.py:17
  122.3 4.6 %cholesky.44 = f32[50,50]{1,0:T(8,128)S(1)} custom-call(f32[50,50]{1,0:T(8,128)S(1)} %fusion.54), custom_call_target="Cholesky" | custom-call | tf_op jit(solution)/shard_map/jit(cholesky)/cholesky | solution.py:51
  127.5 0.7 fusion.47
  128.2 3.8 %custom-call.11 = f32[1,50,50]{1,2,0:T(8,128)S(1)} custom-call(f32[1,50,50]{2,1,0:T(8,128)S(1)} %fusion.47), custom_call_target="InvertDiagBlocksLowerTriangular" | custom-call | tf_op jit(solution)/shard_map/triangular_solve/custom-call.2 | solution.py:53
  132.7 24.8 %all_to_all.25 = bf16[64,4,3,128]{3,1,2,0:T(4,128)(2,1)S(1)} all-to-all(bf16[64,4,3,128]{3,1,2,0:T(4,128)(2,1)S(1)} %broadcast_in_dim.54), channel_id=1, replica_groups=mesh['fluid_0'=8,'fluid_1'=4,'fluid_2'=2,'solid'=8] {'fluid_0','fluid_1'..., dimensions={0} | all-to-all | bytes 393216 | tf_op jit(solution)/shard_map/all_to_all | solution.py:23
  157.8 1.7 fusion.8
  160.0 0.7 copy.54
  160.8 4.5 %all-to-all-start.3 = ((bf16[64,4,3,128]{3,1,2,0:T(4,128)(2,1)}), bf16[64,4,3,128]{3,1,2,0:T(4,128)(2,1)S(1)}, u32[]{:S(2)}, u32[]{:S(2)}) async-start(bf16[64,4,3,128]{3,1,2,0:T(4,128)(2,1)} %copy.54), calls=%async_computation.3 | async-start | bytes 393216 | tf_op jit(solution)/shard_map/all_to_all | solution.py:44
  165.4 12.0 %all-to-all-done.3 = bf16[64,4,3,128]{3,1,2,0:T(4,128)(2,1)S(1)} async-done(((bf16[64,4,3,128]{3,1,2,0:T(4,128)(2,1)}), bf16[64,4,3,128]{3,1,2,0:T(4,128)(2,1)S(1)}, u32[]{:S(2)}, u32[]{:S(2)}) %all-to-all-start.3) | async-done | bytes 196640 | tf_op jit(solution)/shard_map/all_to_all | solution.py:44
  178.4 11.9 %all-reduce.2 = (f32[50]{0:T(128)S(1)}, f32[50]{0:T(128)S(1)}) all-reduce(f32[50]{0:T(128)S(1)} %convolution_bitcast_fusion.1, f32[50]{0:T(128)S(1)} %convolution_bitcast_fusion.2), channel_id=1, replica_groups=mesh['fluid_0'=8,'fluid_1'=4,'fluid_2'=2,'solid'=8] {'fluid_0'}, use_global_device_ids=true, to_apply=%region_18.0 | all-reduce | flops 100 | bytes 800 | tf_op jit(solution)/shard_map/psum | solution.py:17
  190.2 6.5 %all-reduce.4 = (f32[50]{0:T(128)S(1)}, f32[50]{0:T(128)S(1)}) all-reduce(f32[50]{0:T(128)S(1)} %get-tuple-element.15, f32[50]{0:T(128)S(1)} %get-tuple-element.16), channel_id=1, replica_groups=mesh['fluid_0'=8,'fluid_1'=4,'fluid_2'=2,'solid'=8] {'fluid_1'}, use_global_device_ids=true, to_apply=%region_19.23 | all-reduce | flops 100 | bytes 800 | tf_op jit(solution)/shard_map/psum | solution.py:17
  196.8 8.5 %all-reduce.6 = (f32[50]{0:T(128)S(1)}, f32[50]{0:T(128)S(1)}) all-reduce(f32[50]{0:T(128)S(1)} %get-tuple-element.19, f32[50]{0:T(128)S(1)} %get-tuple-element.20), channel_id=1, replica_groups=mesh['fluid_0'=8,'fluid_1'=4,'fluid_2'=2,'solid'=8] {'fluid_2'}, use_global_device_ids=true, to_apply=%region_20.24 | all-reduce | flops 100 | bytes 800 | tf_op jit(solution)/shard_map/psum | solution.py:17
  205.3 10.8 %all-reduce = (f32[50,1]{0,1:T(1,128)S(1)}, f32[50]{0:T(128)S(1)}) all-reduce(f32[50,1]{0,1:T(1,128)S(1)} %bitcast.165, f32[50]{0:T(128)S(1)} %get-tuple-element.24), channel_id=1, replica_groups=mesh['fluid_0'=8,'fluid_1'=4,'fluid_2'=2,'solid'=8] {'solid'}, use_global_device_ids=true, to_apply=%region_21.25 | all-reduce | flops 100 | bytes 800 | tf_op jit(solution)/shard_map/psum | solution.py:17
  216.1 0.7 select_reduce_fusion.2
  217.7 4.6 %cholesky.55 = f32[50,50]{1,0:T(8,128)S(1)} custom-call(f32[50,50]{1,0:T(8,128)S(1)} %fusion.51), custom_call_target="Cholesky" | custom-call | tf_op jit(solution)/shard_map/jit(cholesky)/cholesky | solution.py:51
  223.0 0.7 fusion.48
  223.6 3.8 %custom-call.13 = f32[1,50,50]{1,2,0:T(8,128)S(1)} custom-call(f32[1,50,50]{2,1,0:T(8,128)S(1)} %fusion.48), custom_call_target="InvertDiagBlocksLowerTriangular" | custom-call | tf_op jit(solution)/shard_map/triangular_solve/custom-call.2 | solution.py:53
  228.8 20.7 %all_to_all.26 = bf16[64,4,3,128]{3,1,2,0:T(4,128)(2,1)S(1)} all-to-all(bf16[64,4,3,128]{3,1,2,0:T(4,128)(2,1)S(1)} %broadcast_in_dim.61), channel_id=1, replica_groups=mesh['fluid_0'=8,'fluid_1'=4,'fluid_2'=2,'solid'=8] {'fluid_0','fluid_1'..., dimensions={0} | all-to-all | bytes 393216 | tf_op jit(solution)/shard_map/all_to_all | solution.py:23
  249.8 0.7 convolution_multiply_fusion
  250.5 0.7 copy.59
  (60 shorter events, 8.3 us)
Async XLA Ops:
  0.6 28.7 %copy-start = (bf16[64,128,128]{2,1,0:T(8,128)(2,1)S(1)}, bf16[64,128,128]{2,1,0:T(8,128)(2,1)}, u32[]{:S(2)}) copy-start(bf16[64,128,128]{2,1,0:T(8,128)(2,1)} %param.17) | copy-start | bytes 6291460
  2.2 26.8 %all-to-all-start = ((bf16[64,4,3,128]{3,1,2,0:T(4,128)(2,1)}), bf16[64,4,3,128]{3,1,2,0:T(4,128)(2,1)S(1)}, u32[]{:S(2)}, u32[]{:S(2)}) async-start(bf16[64,4,3,128]{3,1,2,0:T(4,128)(2,1)} %broadcast_in_dim.50), calls=%async_computation | async-start | bytes 393216 | tf_op jit(solution)/shard_map/all_to_all | solution.py:23
  29.3 8.4 %copy-start.1 = (f32[50,1,4,3,128]{4,2,3,1,0:T(4,128)S(1)}, f32[50,1,4,3,128]{4,2,3,1,0:T(4,128)}, u32[]{:S(2)}) copy-start(f32[50,1,4,3,128]{4,2,3,1,0:T(4,128)} %param.23) | copy-start | bytes 921604
  29.4 20.7 %copy-start.5 = (f32[1,4,3,128]{3,1,2,0:T(4,128)S(1)}, f32[1,4,3,128]{3,1,2,0:T(4,128)}, u32[]{:S(2)}) copy-start(f32[1,4,3,128]{3,1,2,0:T(4,128)} %param.21) | copy-start | bytes 18436
  29.4 20.7 %copy-start.6 = (f32[1,4,3,128]{3,1,2,0:T(4,128)S(1)}, f32[1,4,3,128]{3,1,2,0:T(4,128)}, u32[]{:S(2)}) copy-start(f32[1,4,3,128]{3,1,2,0:T(4,128)} %param.22) | copy-start | bytes 18436
  32.1 100.2 %copy-start.2 = (f32[50,1,4,3,128]{4,2,3,1,0:T(4,128)S(1)}, f32[50,1,4,3,128]{4,2,3,1,0:T(4,128)}, u32[]{:S(2)}) copy-start(f32[50,1,4,3,128]{4,2,3,1,0:T(4,128)} %param.24) | copy-start | bytes 921604
  32.1 125.8 %copy-start.3 = (f32[64,3,128]{2,0,1:T(8,128)S(1)}, f32[64,3,128]{2,0,1:T(8,128)}, u32[]{:S(2)}) copy-start(f32[64,3,128]{2,0,1:T(8,128)} %param.15) | copy-start | bytes 294916
  32.1 125.8 %copy-start.4 = (f32[64,3,128]{2,0,1:T(8,128)S(1)}, f32[64,3,128]{2,0,1:T(8,128)}, u32[]{:S(2)}) copy-start(f32[64,3,128]{2,0,1:T(8,128)} %param.16) | copy-start | bytes 294916
  33.3 16.6 %all-to-all-start.1 = ((bf16[64,4,3,128]{3,1,2,0:T(4,128)(2,1)}), bf16[64,4,3,128]{3,1,2,0:T(4,128)(2,1)S(1)}, u32[]{:S(2)}, u32[]{:S(2)}) async-start(bf16[64,4,3,128]{3,1,2,0:T(4,128)(2,1)} %copy.44), calls=%async_computation.1 | async-start | bytes 393216 | tf_op jit(solution)/shard_map/all_to_all | solution.py:44
  160.8 16.6 %all-to-all-start.3 = ((bf16[64,4,3,128]{3,1,2,0:T(4,128)(2,1)}), bf16[64,4,3,128]{3,1,2,0:T(4,128)(2,1)S(1)}, u32[]{:S(2)}, u32[]{:S(2)}) async-start(bf16[64,4,3,128]{3,1,2,0:T(4,128)(2,1)} %copy.54), calls=%async_computation.3 | async-start | bytes 393216 | tf_op jit(solution)/shard_map/all_to_all | solution.py:44
where the time goes:
time: 252 us; the launch traced here: 251 us
  blocking collectives  154 us (61%)
  waiting for transfers between devices  34.4 us (14%)
  starting transfers between devices  23.8 us (9%)
  other arithmetic  23.5 us (9%)
  matrix products  9.37 us (4%)
  local copies, waits for them, and re-layouts  3.67 us (1%)
  between operations  2.85 us (1%)
    psum x8, blocking collectives, over_axes(): x = lax.psum(x, axis)  108 us
    all_to_all x2, blocking collectives, sent_to_all(): return lax.all_to_all(copies, axis, split_axis=0, concat_axis=0, tiled=True)  45.6 us
    all_to_all x2, waiting for transfers between devices, sum_at_owner(): parts = lax.all_to_all(in_blocks(x, dim, count), axis, 0, 0, tiled=True)  23.7 us
    all_to_all x1, starting transfers between devices, sent_to_all(): return lax.all_to_all(copies, axis, split_axis=0, concat_axis=0, tiled=True)  14.8 us
    all_to_all x1, waiting for transfers between devices, sent_to_all(): return lax.all_to_all(copies, axis, split_axis=0, concat_axis=0, tiled=True)  10.7 us
    another operation x6, other arithmetic, solve_small(): jnp.linalg.cholesky(gram_matrix + ridge * jnp.eye(order, dtype=gram_matri...  10.5 us
    another operation x4, other arithmetic, solve_small(): lax.linalg.triangular_solve(factor, halfway, left_side=True, lower=True,...  8.96 us
    all_to_all x2, starting transfers between devices, sum_at_owner(): parts = lax.all_to_all(in_blocks(x, dim, count), axis, 0, 0, tiled=True)  8.93 us
  transfers between devices with their start and end apart: 3, of which 3 were waited for; matrix products, arithmetic and copies ran while one was open for 0% of the time, Pallas kernels for 0%

commit v1 on v0

v1 whole, which is shorter than its diff:
```python
import jax
import jax.numpy as jnp
from jax import lax
from jax.experimental import pallas as pl
from jax.experimental.pallas import tpu as pltpu
from jax.sharding import Mesh
from jax.sharding import PartitionSpec as P

ITERS = 2
HIST = 50
RIDGE_SHARE = 0.01
ALL = ("z", "x", "c", "solid")
FLUID = ("z", "x", "c")
NEAR = ("c", "solid")
FAR = ("z", "x")
ROWS = 56
RHS = 64
HIGHEST = lax.Precision.HIGHEST


def exchange(x, axes):
    return lax.all_to_all(x, axes, split_axis=0, concat_axis=0, tiled=True)


def sent_to_all(x, axes):
    return exchange(jnp.broadcast_to(x, (lax.axis_size(axes), *x.shape)), axes)


def three_pieces(x):
    high = lax.reduce_precision(x, 8, 7)
    rest = x - high
    middle = lax.reduce_precision(rest, 8, 7)
    return high, middle, rest - middle


def solve_kernel(system_ref, out_ref):
    a = system_ref[...]
    rows = lax.broadcasted_iota(jnp.int32, a.shape, 0)
    lanes = lax.broadcasted_iota(jnp.int32, a.shape, 1)
    diag = (rows == lanes) & (rows < HIST)
    trace = jnp.sum(jnp.where(diag, a, 0.0))
    a = a + jnp.where(diag, RIDGE_SHARE * trace / HIST, 0.0)
    for k in range(HIST):
        row = a[k : k + 1, :]
        row = row / row[:, k : k + 1]
        a = jnp.where(rows == k, row, a - a[:, k : k + 1] * row)
    out_ref[...] = -jnp.broadcast_to(a[:, RHS : RHS + 1], a.shape)


def solve_small(gram_matrix, right_side):
    system = jnp.zeros((ROWS, 128), jnp.float32)
    system = system.at[:HIST, :HIST].set(gram_matrix)
    system = system.at[:HIST, RHS].set(right_side)
    solved = pl.pallas_call(
        solve_kernel,
        out_shape=jax.ShapeDtypeStruct((ROWS, 128), jnp.float32),
        in_specs=[pl.BlockSpec(memory_space=pltpu.VMEM)],
        out_specs=pl.BlockSpec(memory_space=pltpu.VMEM),
        name="solve",
    )(system)
    return solved[:HIST, 0]


def body(
    fluid_load,
    stiffness,
    mapping,
    live_count,
    dest_device,
    local_block,
    compliance,
    start_disp,
    residual_history,
    update_history,
):
    blocks = mapping.shape[0]
    sub_blocks = compliance.shape[1]
    peers = lax.axis_size(FLUID)
    far = lax.axis_size(FAR)
    near = lax.axis_size(NEAR)
    alive = (jnp.arange(blocks) < live_count[0]).astype(jnp.float32)[:, None, None]
    dest = dest_device[:, 0]
    order = jnp.arange(blocks)
    earlier = (dest[:, None] == dest[None, :]) & (order[None, :] < order[:, None])
    place = dest * 2 + jnp.sum(earlier, axis=1)
    place_hot = (place[:, None] == jnp.arange(2 * peers)[None, :]).astype(jnp.bfloat16)
    names = jnp.sum(
        jnp.where(
            place[:, None] == jnp.arange(2 * peers)[None, :], local_block[:, None] + 1, 0
        ),
        axis=0,
    ).astype(jnp.float32)

    def on_fluid(picked):
        return jnp.einsum(
            "bjn,bcj->bcn",
            mapping,
            picked.astype(jnp.bfloat16),
            preferred_element_type=jnp.float32,
        ) * alive

    def places_filled(picked):
        force = (alive * (fluid_load - stiffness * on_fluid(picked))).astype(jnp.bfloat16)
        contrib = jnp.einsum("bjn,bcn->bcj", mapping, force, preferred_element_type=jnp.float32)
        filled = jnp.einsum(
            "bp,bcj->pcj",
            place_hot,
            contrib.astype(jnp.bfloat16),
            preferred_element_type=jnp.float32,
        )
        return filled.astype(jnp.bfloat16).reshape(peers, 6, 128)

    def summed_at_owner(got, names_hot):
        return jnp.einsum(
            "pk,pcj->kcj",
            names_hot,
            got[:, :6].reshape(2 * peers, 3, 128),
            preferred_element_type=jnp.float32,
        )[None]

    def picked_by_places(struct_disp, names_hot):
        packed = struct_disp[0].astype(jnp.bfloat16)
        chosen = jnp.einsum(
            "pk,kcj->pcj", names_hot, packed, preferred_element_type=jnp.float32
        ).astype(jnp.bfloat16)
        got = exchange(chosen.reshape(peers, 6, 128), FLUID)
        return jnp.einsum(
            "bp,pcj->bcj",
            place_hot,
            got.reshape(2 * peers, 3, 128),
            preferred_element_type=jnp.float32,
        )

    basis = residual_history.reshape(HIST, -1)
    gram_local = jnp.dot(basis, basis.T, precision=HIGHEST)
    pieces = three_pieces(jnp.pad(gram_local, ((0, peers - HIST), (0, 64 - HIST))))
    side = jnp.concatenate(
        [pieces[0], pieces[1], pieces[2], jnp.zeros((peers, 62)), names.reshape(peers, 2)], axis=1
    )
    side = side.astype(jnp.bfloat16).reshape(peers, 2, 128)

    whole = sent_to_all(start_disp[0].astype(jnp.bfloat16).reshape(sub_blocks, 3 * 128), FLUID)
    target = dest * sub_blocks + local_block
    target_hot = (target[:, None] == jnp.arange(peers * sub_blocks)[None, :]).astype(jnp.bfloat16)
    picked = jnp.dot(
        target_hot,
        whole.reshape(peers * sub_blocks, 3 * 128),
        preferred_element_type=jnp.float32,
    ).reshape(blocks, 3, 128)

    got = exchange(jnp.concatenate([places_filled(picked), side], axis=1), FLUID)
    names_got = got[:, 7, 126:].reshape(2 * peers)
    names_hot = (
        names_got[:, None] == jnp.arange(1, sub_blocks + 1).astype(jnp.bfloat16)[None, :]
    ).astype(jnp.bfloat16)
    row_pieces = jnp.sum(got[:, 6:8].astype(jnp.float32), axis=0)
    gram_row = row_pieces[0, :64] + row_pieces[0, 64:] + row_pieces[1, :64]
    gram_row = jnp.where(jnp.arange(64) < HIST, gram_row, 0.0)

    image = compliance * summed_at_owner(got, names_hot)
    residual = image - start_disp
    right_local = jnp.dot(basis, residual.reshape(-1), precision=HIGHEST)
    line = jnp.concatenate([jnp.pad(right_local, (0, 64 - HIST)), gram_row])
    near_got = sent_to_all(line, NEAR).reshape(2, near // 2, 128)
    near_rows = jnp.sum(near_got[:, :, 64:], axis=1).reshape(1, 128)
    near_right = jnp.sum(near_got, axis=(0, 1))[None]
    far_got = sent_to_all(jnp.concatenate([near_right, near_rows], axis=0), FAR)
    gram = far_got[:, 1].reshape(peers, 64)[:HIST, :HIST]
    right = jnp.sum(far_got[:, 0, :HIST], axis=0)
    coefficients = solve_small(gram, right)
    struct_disp = image + jnp.tensordot(coefficients, update_history, axes=1, precision=HIGHEST)

    filled = places_filled(picked_by_places(struct_disp, names_hot))
    got = exchange(filled, FLUID)
    last_image, last_residual = image, residual
    image = compliance * summed_at_owner(got, names_hot)
    residual = image - struct_disp
    newest = residual - last_residual
    both = jnp.stack([residual.reshape(-1), newest.reshape(-1)])
    columns = jnp.concatenate([basis[1:], newest.reshape(1, -1)], axis=0)
    sums = jnp.pad(jnp.dot(both, columns.T, precision=HIGHEST), ((0, 0), (0, 64 - HIST)))
    near_got = sent_to_all(sums.reshape(1, 128), NEAR)
    far_got = sent_to_all(jnp.sum(near_got, axis=0), FAR)
    sums = jnp.sum(far_got, axis=0).reshape(2, 64)[:, :HIST]
    right, row = sums[0], sums[1]
    gram = jnp.concatenate(
        [jnp.concatenate([gram[1:, 1:], row[:-1, None]], 1), row[None, :]], 0
    )
    coefficients = solve_small(gram, right)
    struct_disp = (
        image
        + jnp.tensordot(coefficients[:-1], update_history[1:], axes=1, precision=HIGHEST)
        + coefficients[-1] * (image - last_image)
    )
    final_disp = on_fluid(picked_by_places(struct_disp, names_hot))
    return (struct_disp, final_disp)


def solution(mesh):
    split = Mesh(mesh.devices.reshape(8, 4, 2, mesh.shape["solid"]), ALL)
    in_specs = (
        P(ALL, None, None),
        P(ALL, None, None),
        P(ALL, None, None),
        P(ALL),
        P(ALL, None),
        P(ALL),
        P("solid", FLUID, None, None),
        P("solid", FLUID, None, None),
        P(None, "solid", FLUID, None, None),
        P(None, "solid", FLUID, None, None),
    )
    out_specs = (P("solid", FLUID, None, None), P(ALL, None, None))
    return jax.shard_map(body, mesh=split, in_specs=in_specs, out_specs=out_specs, check_vma=False)
```

time: 252 us -> 182 us (0.72)
  blocking collectives: 154 us -> 42.6 us
  waiting for transfers between devices: 34.4 us -> 52.2 us
  starting transfers between devices: 23.8 us -> 38.9 us
  other arithmetic: 23.5 us -> 9.72 us
  local copies, waits for them, and re-layouts: 3.67 us -> 15.3 us
  Pallas kernels: 0 us -> 11.5 us
    psum x8 -> x0, blocking collectives: 108 us -> none  [over_axes(): x = lax.psum(x, axis)]
    all_to_all x3 -> x6, waiting for transfers between devices: 34.4 us -> 52.2 us  [exchange(): return lax.all_to_all(x, axes, split_axis=0, concat_axis=0, tiled=True)]
    all_to_all x3 -> x6, starting transfers between devices: 23.8 us -> 38.9 us  [exchange(): return lax.all_to_all(x, axes, split_axis=0, concat_axis=0, tiled=True)]
    another operation x13 -> x6, other arithmetic: 19.6 us -> 4.6 us  [the longest x6 10.5 us: solve_small(): jnp.linalg.cholesky(gram_matrix + ridge * jnp.eye(order, dtype=gram_matri...]
    pallas_call x0 -> x2, Pallas kernels: none -> 11.5 us  [solve_small(): pl.pallas_call(solve_kernel, out_shape=jax.ShapeDtypeStruct((ROWS, 128),...]
    scatter x0 -> x3, local copies, waits for them, and re-layouts: none -> 3.69 us  [the longest x2 3.68 us: solve_small(): system = system.at[:HIST, RHS].set(right_side)]
    slice x3 -> x10, local copies, waits for them, and re-layouts: 0.14 us -> 3.5 us  [the longest x1 1.2 us: body(): coefficients[-1] * (image - last_image)]
    all_to_all x2 -> x3, blocking collectives: 45.6 us -> 42.6 us  [exchange(): return lax.all_to_all(x, axes, split_axis=0, concat_axis=0, tiled=True)]
  transfers between devices with their start and end apart: 3 -> 6, of which waited for: 3 -> 6; matrix products, arithmetic and copies ran while one was open for 0% -> 3% of each run, Pallas kernels for 0% -> 0%
where the time goes in v1:
time: 182 us; the launch traced here: 181 us
  waiting for transfers between devices  52.2 us (29%)
  blocking collectives  42.6 us (23%)
  starting transfers between devices  38.9 us (21%)
  local copies, waits for them, and re-layouts  15.3 us (8%)
  Pallas kernels  11.5 us (6%)
  other arithmetic  9.72 us (5%)
  matrix products  9.13 us (5%)
    all_to_all x6, waiting for transfers between devices, exchange(): return lax.all_to_all(x, axes, split_axis=0, concat_axis=0, tiled=True)  52.2 us
    all_to_all x3, blocking collectives, exchange(): return lax.all_to_all(x, axes, split_axis=0, concat_axis=0, tiled=True)  42.6 us
    all_to_all x6, starting transfers between devices, exchange(): return lax.all_to_all(x, axes, split_axis=0, concat_axis=0, tiled=True)  38.9 us
    pallas_call x2, Pallas kernels, solve_small(): pl.pallas_call(solve_kernel, out_shape=jax.ShapeDtypeStruct((ROWS, 128),...  11.5 us
    another operation x6, other arithmetic  4.6 us
    scatter x2, local copies, waits for them, and re-layouts, solve_small(): system = system.at[:HIST, RHS].set(right_side)  3.68 us
  transfers between devices with their start and end apart: 6, of which 6 were waited for; matrix products, arithmetic and copies ran while one was open for 3% of the time, Pallas kernels for 0%

profile of v1, /device:TPU:1, one launch (start us, length us, event | category | flops | bytes accessed | tf_op | source)
XLA Modules:
  0.0 181.2 jit_solution(13075794882338413819)
XLA Ops:
  0.7 0.8 convert_bitcast_fusion
  1.5 0.7 broadcast_in_dim.57
  2.2 14.8 %all-to-all-start = ((bf16[64,4,384]{2,1,0:T(4,128)(2,1)}), bf16[64,4,384]{2,1,0:T(4,128)(2,1)S(1)}, u32[]{:S(2)}, u32[]{:S(2)}) async-start(bf16[64,4,384]{2,1,0:T(4,128)(2,1)} %broadcast_in_dim.57), calls=%async_computation | async-start | bytes 393216 | tf_op jit(solution)/shard_map/all_to_all | solution.py:22
  17.1 0.9 convert_reduce_fusion.1
  20.2 1.5 convolution_bitcast_fusion
  21.9 7.2 %all-to-all-done = bf16[64,4,384]{2,1,0:T(4,128)(2,1)S(1)} async-done(((bf16[64,4,384]{2,1,0:T(4,128)(2,1)}), bf16[64,4,384]{2,1,0:T(4,128)(2,1)S(1)}, u32[]{:S(2)}, u32[]{:S(2)}) %all-to-all-start) | async-done | bytes 196640 | tf_op jit(solution)/shard_map/all_to_all | solution.py:22
  29.6 1.7 convolution_convert_fusion.5
  31.8 0.7 pad_maximum_fusion
  32.5 4.5 %all-to-all-start.1 = ((bf16[64,8,128]{2,1,0:T(8,128)(2,1)}), bf16[64,8,128]{2,1,0:T(8,128)(2,1)S(1)}, u32[]{:S(2)}, u32[]{:S(2)}) async-start(bf16[64,8,128]{2,1,0:T(8,128)(2,1)} %pad_maximum_fusion), calls=%async_computation.1 | async-start | bytes 262144 | tf_op jit(solution)/shard_map/all_to_all | solution.py:22
  37.6 10.7 %all-to-all-done.1 = bf16[64,8,128]{2,1,0:T(8,128)(2,1)S(1)} async-done(((bf16[64,8,128]{2,1,0:T(8,128)(2,1)}), bf16[64,8,128]{2,1,0:T(8,128)(2,1)S(1)}, u32[]{:S(2)}, u32[]{:S(2)}) %all-to-all-start.1) | async-done | bytes 131104 | tf_op jit(solution)/shard_map/all_to_all | solution.py:22
  50.1 7.5 %all-to-all-start.2 = ((f32[16,1,128]{2,1,0:T(1,128)}), f32[16,1,128]{2,1,0:T(1,128)S(1)}, u32[]{:S(2)}, u32[]{:S(2)}) async-start(f32[16,1,128]{2,1,0:T(1,128)} %broadcast_in_dim.63), calls=%async_computation.2 | async-start | bytes 16384 | tf_op jit(solution)/shard_map/all_to_all | solution.py:22
  57.7 6.9 %all-to-all-done.2 = f32[16,1,128]{2,1,0:T(1,128)S(1)} async-done(((f32[16,1,128]{2,1,0:T(1,128)}), f32[16,1,128]{2,1,0:T(1,128)S(1)}, u32[]{:S(2)}, u32[]{:S(2)}) %all-to-all-start.2) | async-done | bytes 8224 | tf_op jit(solution)/shard_map/all_to_all | solution.py:22
  65.4 3.9 %all-to-all-start.3 = ((f32[32,2,128]{2,1,0:T(2,128)}), f32[32,2,128]{2,1,0:T(2,128)S(1)}, u32[]{:S(2)}, u32[]{:S(2)}) async-start(f32[32,2,128]{2,1,0:T(2,128)} %broadcast_in_dim.65), calls=%async_computation.3 | async-start | bytes 65536 | tf_op jit(solution)/shard_map/all_to_all | solution.py:22
  69.8 8.0 %all-to-all-done.3 = f32[32,2,128]{2,1,0:T(2,128)S(1)} async-done(((f32[32,2,128]{2,1,0:T(2,128)}), f32[32,2,128]{2,1,0:T(2,128)S(1)}, u32[]{:S(2)}, u32[]{:S(2)}) %all-to-all-start.3) | async-done | bytes 32800 | tf_op jit(solution)/shard_map/all_to_all | solution.py:22
  78.2 2.0 %dynamic-slice_select_fusion.1 = f32[50,1]{1,0:T(8,128)S(1)} fusion(f32[50,1]{1,0:T(8,128)S(1)} %copy.133, s32[]{:T(128)} %bitcast.23, s32[]{:T(128)} %bitcast.24, pred[]{:T(512)} %and_reduce_fusion, f32[50,50]{1,0:T(8,128)S(1)} %slice.179), kind=kLoop, calls=%fused_computation.76 | loop fusion | flops 50 | bytes 10409 | tf_op jit(solution)/shard_map/select.5
  80.2 1.8 %scatter.15.system_ref = f32[56,128]{1,0:T(8,128)S(1)} dynamic-update-slice(f32[56,128]{1,0:T(8,128)S(1)} %scatter.14, f32[50,1]{1,0:T(8,128)S(1)} %dynamic-slice_select_fusion.1, s32[]{:T(128)} %bitcast.23, s32[]{:T(128)} %bitcast.24) | dynamic-update-slice | bytes 404 | tf_op jit(solution)/shard_map/scatter | solution.py:53
  82.6 5.8 %solve.2 = f32[56,128]{1,0:T(8,128)} custom-call(f32[56,128]{1,0:T(8,128)} %copy-done.6), custom_call_target="tpu_custom_call" | custom-call | tf_op jit(solution)/shard_map/solve/pallas_call | solution.py:54
  88.4 0.9 slice_reduce_fusion.2
  90.1 16.4 %all_to_all.46 = bf16[64,6,128]{2,1,0:T(8,128)(2,1)S(1)} all-to-all(bf16[64,6,128]{2,1,0:T(8,128)(2,1)S(1)} %reshape.238), channel_id=1, replica_groups=mesh['z'=8,'x'=4,'c'=2,'solid'=8] {'z','x','c'}, dimensions={0} | all-to-all | bytes 196608 | tf_op jit(solution)/shard_map/all_to_all | solution.py:22
  106.8 1.7 convolution_convert_fusion.4
  108.9 0.7 reshape.240
  109.6 4.5 %all-to-all-start.5 = ((bf16[64,6,128]{2,1,0:T(8,128)(2,1)}), bf16[64,6,128]{2,1,0:T(8,128)(2,1)S(1)}, u32[]{:S(2)}, u32[]{:S(2)}) async-start(bf16[64,6,128]{2,1,0:T(8,128)(2,1)} %reshape.240), calls=%async_computation.5 | async-start | bytes 262144 | tf_op jit(solution)/shard_map/all_to_all | solution.py:22
  114.4 11.0 %all-to-all-done.5 = bf16[64,6,128]{2,1,0:T(8,128)(2,1)S(1)} async-done(((bf16[64,6,128]{2,1,0:T(8,128)(2,1)}), bf16[64,6,128]{2,1,0:T(8,128)(2,1)S(1)}, u32[]{:S(2)}, u32[]{:S(2)}) %all-to-all-start.5) | async-done | bytes 98336 | tf_op jit(solution)/shard_map/all_to_all | solution.py:22
  126.2 9.8 %all_to_all.47 = f32[16,1,128]{2,1,0:T(1,128)S(1)} all-to-all(f32[16,1,128]{2,1,0:T(1,128)S(1)} %broadcast_in_dim.67), channel_id=1, replica_groups=mesh['z'=8,'x'=4,'c'=2,'solid'=8] {'c','solid'}, dimensions={0} | all-to-all | bytes 16384 | tf_op jit(solution)/shard_map/all_to_all | solution.py:22
  136.6 3.8 %all-to-all-start.7 = ((f32[32,1,128]{2,1,0:T(1,128)}), f32[32,1,128]{2,1,0:T(1,128)S(1)}, u32[]{:S(2)}, u32[]{:S(2)}) async-start(f32[32,1,128]{2,1,0:T(1,128)} %broadcast_in_dim.68), calls=%async_computation.7 | async-start | bytes 32768 | tf_op jit(solution)/shard_map/all_to_all | solution.py:22
  140.6 8.4 %all-to-all-done.7 = f32[32,1,128]{2,1,0:T(1,128)S(1)} async-done(((f32[32,1,128]{2,1,0:T(1,128)}), f32[32,1,128]{2,1,0:T(1,128)S(1)}, u32[]{:S(2)}, u32[]{:S(2)}) %all-to-all-start.7) | async-done | bytes 16416 | tf_op jit(solution)/shard_map/all_to_all | solution.py:22
  149.4 2.0 %dynamic-slice_select_fusion = f32[50,1]{1,0:T(8,128)S(1)} fusion(f32[50,1]{1,0:T(8,128)S(1)} %copy.148, f32[56,128]{1,0:T(8,128)S(1)} %select_maximum_fusion, s32[]{:T(128)} %bitcast.23, s32[]{:T(128)} %bitcast.24, pred[]{:T(512)} %and_reduce_fusion), kind=kLoop, calls=%fused_computation.75 | loop fusion | flops 50 | bytes 609 | tf_op jit(solution)/shard_map/select.7
  151.4 1.8 %scatter.19.system_ref = f32[56,128]{1,0:T(8,128)S(1)} dynamic-update-slice(f32[56,128]{1,0:T(8,128)S(1)} %select_maximum_fusion, f32[50,1]{1,0:T(8,128)S(1)} %dynamic-slice_select_fusion, s32[]{:T(128)} %bitcast.23, s32[]{:T(128)} %bitcast.24) | dynamic-update-slice | bytes 404 | tf_op jit(solution)/shard_map/scatter | solution.py:53
  153.9 5.8 %solve.3 = f32[56,128]{1,0:T(8,128)} custom-call(f32[56,128]{1,0:T(8,128)} %copy-done.5), custom_call_target="tpu_custom_call" | custom-call | tf_op jit(solution)/shard_map/solve/pallas_call | solution.py:54
  159.6 1.2 slice.184
  160.8 0.9 slice_reduce_fusion.1
  163.2 16.4 %all_to_all.48 = bf16[64,6,128]{2,1,0:T(8,128)(2,1)S(1)} all-to-all(bf16[64,6,128]{2,1,0:T(8,128)(2,1)S(1)} %reshape.246), channel_id=1, replica_groups=mesh['z'=8,'x'=4,'c'=2,'solid'=8] {'z','x','c'}, dimensions={0} | all-to-all | bytes 196608 | tf_op jit(solution)/shard_map/all_to_all | solution.py:22
  (103 shorter events, 14.8 us)
Async XLA Ops:
  0.6 28.9 %copy-start = (bf16[64,128,128]{2,1,0:T(8,128)(2,1)S(1)}, bf16[64,128,128]{2,1,0:T(8,128)(2,1)}, u32[]{:S(2)}) copy-start(bf16[64,128,128]{2,1,0:T(8,128)(2,1)} %param.20) | copy-start | bytes 6291460
  0.6 28.8 %copy-start.4 = (f32[64,3,128]{2,0,1:T(8,128)S(1)}, f32[64,3,128]{2,0,1:T(8,128)}, u32[]{:S(2)}) copy-start(f32[64,3,128]{2,0,1:T(8,128)} %param.19) | copy-start | bytes 294916
  0.7 28.8 %copy-start.3 = (f32[64,3,128]{2,0,1:T(8,128)S(1)}, f32[64,3,128]{2,0,1:T(8,128)}, u32[]{:S(2)}) copy-start(f32[64,3,128]{2,0,1:T(8,128)} %param.18) | copy-start | bytes 294916
  2.2 26.8 %all-to-all-start = ((bf16[64,4,384]{2,1,0:T(4,128)(2,1)}), bf16[64,4,384]{2,1,0:T(4,128)(2,1)S(1)}, u32[]{:S(2)}, u32[]{:S(2)}) async-start(bf16[64,4,384]{2,1,0:T(4,128)(2,1)} %broadcast_in_dim.57), calls=%async_computation | async-start | bytes 393216 | tf_op jit(solution)/shard_map/all_to_all | solution.py:22
  29.5 7.5 %copy-start.10 = (s32[2]{0:T(128)S(1)}, s32[2]{0:T(128)}, u32[]{:S(2)}) copy-start(s32[2]{0:T(128)} %constant.100.clone.1) | copy-start | bytes 28
  29.5 19.3 %copy-start.7 = (f32[1,4,3,128]{3,1,2,0:T(4,128)S(1)}, f32[1,4,3,128]{3,1,2,0:T(4,128)}, u32[]{:S(2)}) copy-start(f32[1,4,3,128]{3,1,2,0:T(4,128)} %param.25) | copy-start | bytes 18436
  29.5 19.3 %copy-start.9 = (f32[1,4,3,128]{3,1,2,0:T(4,128)S(1)}, f32[1,4,3,128]{3,1,2,0:T(4,128)}, u32[]{:S(2)}) copy-start(f32[1,4,3,128]{3,1,2,0:T(4,128)} %param.24) | copy-start | bytes 18436
  29.5 19.5 %copy-start.1 = (f32[50,1,4,3,128]{4,2,3,1,0:T(4,128)S(1)}, f32[50,1,4,3,128]{4,2,3,1,0:T(4,128)}, u32[]{:S(2)}) copy-start(f32[50,1,4,3,128]{4,2,3,1,0:T(4,128)} %param.26) | copy-start | bytes 921604
  31.3 58.0 %copy-start.2 = (f32[50,1,4,3,128]{4,2,3,1,0:T(4,128)S(1)}, f32[50,1,4,3,128]{4,2,3,1,0:T(4,128)}, u32[]{:S(2)}) copy-start(f32[50,1,4,3,128]{4,2,3,1,0:T(4,128)} %param.27) | copy-start | bytes 921604
  32.5 15.8 %all-to-all-start.1 = ((bf16[64,8,128]{2,1,0:T(8,128)(2,1)}), bf16[64,8,128]{2,1,0:T(8,128)(2,1)S(1)}, u32[]{:S(2)}, u32[]{:S(2)}) async-start(bf16[64,8,128]{2,1,0:T(8,128)(2,1)} %pad_maximum_fusion), calls=%async_computation.1 | async-start | bytes 262144 | tf_op jit(solution)/shard_map/all_to_all | solution.py:22
  50.1 14.4 %all-to-all-start.2 = ((f32[16,1,128]{2,1,0:T(1,128)}), f32[16,1,128]{2,1,0:T(1,128)S(1)}, u32[]{:S(2)}, u32[]{:S(2)}) async-start(f32[16,1,128]{2,1,0:T(1,128)} %broadcast_in_dim.63), calls=%async_computation.2 | async-start | bytes 16384 | tf_op jit(solution)/shard_map/all_to_all | solution.py:22
  65.4 12.5 %all-to-all-start.3 = ((f32[32,2,128]{2,1,0:T(2,128)}), f32[32,2,128]{2,1,0:T(2,128)S(1)}, u32[]{:S(2)}, u32[]{:S(2)}) async-start(f32[32,2,128]{2,1,0:T(2,128)} %broadcast_in_dim.65), calls=%async_computation.3 | async-start | bytes 65536 | tf_op jit(solution)/shard_map/all_to_all | solution.py:22
  82.0 0.6 copy-start.6
  109.6 15.8 %all-to-all-start.5 = ((bf16[64,6,128]{2,1,0:T(8,128)(2,1)}), bf16[64,6,128]{2,1,0:T(8,128)(2,1)S(1)}, u32[]{:S(2)}, u32[]{:S(2)}) async-start(bf16[64,6,128]{2,1,0:T(8,128)(2,1)} %reshape.240), calls=%async_computation.5 | async-start | bytes 262144 | tf_op jit(solution)/shard_map/all_to_all | solution.py:22
  136.6 12.4 %all-to-all-start.7 = ((f32[32,1,128]{2,1,0:T(1,128)}), f32[32,1,128]{2,1,0:T(1,128)S(1)}, u32[]{:S(2)}, u32[]{:S(2)}) async-start(f32[32,1,128]{2,1,0:T(1,128)} %broadcast_in_dim.68), calls=%async_computation.7 | async-start | bytes 32768 | tf_op jit(solution)/shard_map/all_to_all | solution.py:22
  153.2 0.6 copy-start.5
  162.6 18.5 %copy-start.8 = (f32[1,4,3,128]{3,1,2,0:T(4,128)}, f32[1,4,3,128]{3,1,2,0:T(4,128)S(1)}, u32[]{:S(2)}) copy-start(f32[1,4,3,128]{3,1,2,0:T(4,128)S(1)} %fusion.54) | copy-start | bytes 18436

commit v2 on v1

v2 whole, which is shorter than its diff:
```python
import jax
import jax.numpy as jnp
from jax import lax
from jax.experimental import pallas as pl
from jax.experimental.pallas import tpu as pltpu
from jax.sharding import Mesh
from jax.sharding import PartitionSpec as P

HIST = 50
RIDGE_SHARE = 0.01
ALL = ("z", "x", "c", "solid")
FLUID = ("z", "x", "c")
NEAR = ("c", "solid")
FAR = ("z", "x")
COLS = 56
PARTS = 12
WIDE = 64
F32, BF16 = jnp.float32, jnp.bfloat16
HIGHEST = lax.Precision.HIGHEST
VMEM = pl.BlockSpec(memory_space=pltpu.VMEM)
SMEM = pl.BlockSpec(memory_space=pltpu.SMEM)


def exchange(x, axes):
    return lax.all_to_all(x, axes, split_axis=0, concat_axis=0, tiled=True)


def three_pieces(x):
    high = lax.reduce_precision(x, 8, 7)
    rest = x - high
    middle = lax.reduce_precision(rest, 8, 7)
    return high, middle, rest - middle


def call(kernel, name, outs, *args, in_specs=None, scratch=()):
    return pl.pallas_call(
        kernel,
        out_shape=[jax.ShapeDtypeStruct(shape, dtype) for shape, dtype in outs],
        in_specs=in_specs or [VMEM] * len(args),
        out_specs=[VMEM] * len(outs),
        scratch_shapes=list(scratch),
        name=name,
    )(*args)


def dot(a, b, dims=((1,), (0,)), precision=None):
    return lax.dot_general(a, b, (dims, ((), ())), precision=precision, preferred_element_type=F32)


def forces_kernel(x_ref, pick_ref, back_ref, map_ref, load_ref, stiff_ref, side_ref, out_ref, xs, fs, cs):
    blocks = map_ref.shape[0]
    xs[...] = dot(pick_ref[...], x_ref[...].reshape(pick_ref.shape[1], 128))
    for b in range(blocks):
        rows = slice(8 * b, 8 * b + 8)
        u = dot(xs[rows, :].astype(BF16), map_ref[b])
        fs[rows, :] = load_ref[rows, :] - stiff_ref[rows, :] * u
    for b in range(blocks):
        rows = slice(8 * b, 8 * b + 8)
        cs[rows, :] = dot(fs[rows, :].astype(BF16), map_ref[b], ((1,), (1,)))
    filled = dot(back_ref[...], cs[...].astype(BF16))
    out_ref[...] = (filled.reshape(out_ref.shape) + side_ref[...].astype(F32)).astype(BF16)


def final_kernel(live_ref, x_ref, pick_ref, map_ref, out_ref, xs):
    xs[...] = dot(pick_ref[...], x_ref[...].reshape(pick_ref.shape[1], 128))
    for b in range(map_ref.shape[0]):
        u = dot(xs[8 * b : 8 * b + 8, :].astype(BF16), map_ref[b])
        out_ref[b] = u[:3] * jnp.where(b < live_ref[0], 1.0, 0.0)


def lanes_of(shape):
    return lax.broadcasted_iota(jnp.int32, shape, len(shape) - 1)


def rows_of(shape):
    return lax.broadcasted_iota(jnp.int32, shape, 0)


def history_sums(vr_ref, vector):
    acc = vr_ref[0] * vector[0:1, :]
    for m in range(1, PARTS):
        acc = acc + vr_ref[m] * vector[m : m + 1, :]
    return acc


def as_row(first, second):
    gap = jnp.zeros((WIDE - COLS, 128), F32)
    stacked = jnp.concatenate([first, gap, second, gap], axis=0)
    return dot(jnp.ones((8, 128), F32), stacked, ((1,), (1,)), HIGHEST)[0:1, :]


def owner_first_kernel(got_ref, comp_ref, x_ref, vr_ref, msg_ref, image_ref, resid_ref, q_ref, qt_ref, xs):
    xs[...] = got_ref[...].astype(F32).reshape(512, 128)
    mark6 = xs[pl.ds(6, 64, stride=8), :]
    mark7 = xs[pl.ds(7, 64, stride=8), :]
    sum6 = jnp.sum(mark6, axis=0, keepdims=True)
    sum7 = jnp.sum(mark7, axis=0, keepdims=True)
    gram_row = sum6 + pltpu.roll(sum6, WIDE, 1) + pltpu.roll(sum7, WIDE, 1)
    spread = (lanes_of((64, 512)) // 8 == rows_of((64, 512))).astype(BF16)
    wide = dot(mark7.astype(BF16), spread, ((0,), (0,)))
    part = rows_of((16, 512))
    row = lanes_of((16, 512)) % 8
    match = part % 3 == row % 3
    q = jnp.where(match & (row < 3), wide[64:80], 0.0)
    q = q + jnp.where(match & (row >= 3) & (row < 6), wide[80:96], 0.0)
    q = q.astype(BF16)
    q_ref[...] = q
    tall = jnp.broadcast_to(
        xs[...].reshape(64, 8, 128)[:, 7:8, :], (64, 8, 128)
    ).reshape(512, 128)
    lane = lanes_of((512, 128))
    row = rows_of((512, 128)) % 8
    match = ((lane % 16) % 3 == row % 3) & (lane % 16 < PARTS)
    match = match & (((row < 3) & (lane // 16 == 4)) | ((row >= 3) & (row < 6) & (lane // 16 == 5)))
    qt_ref[...] = jnp.where(match, tall, 0.0).astype(BF16)
    image = comp_ref[...] * dot(q, xs[...].astype(BF16))
    resid = image - x_ref[...]
    image_ref[...] = image
    resid_ref[...] = resid
    sums = history_sums(vr_ref, resid)
    line = as_row(sums, jnp.zeros_like(sums))
    line = jnp.where(lanes_of(line.shape) < WIDE, line, gram_row)
    msg_ref[...] = jnp.broadcast_to(line.reshape(1, 1, 128), msg_ref.shape)


def owner_next_kernel(got_ref, q_ref, comp_ref, x_ref, last_ref, vr_ref, msg_ref, image_ref):
    got = got_ref[...].astype(F32).reshape(512, 128).astype(BF16)
    image = comp_ref[...] * dot(q_ref[...], got)
    image_ref[...] = image
    resid = image - x_ref[...]
    newest = resid - last_ref[...]
    first = rows_of((COLS, 128)) == 0
    own_right = jnp.sum(newest * resid, axis=0, keepdims=True)
    own_row = jnp.sum(newest * newest, axis=0, keepdims=True)
    right = jnp.where(first, own_right, history_sums(vr_ref, resid))
    row = jnp.where(first, own_row, history_sums(vr_ref, newest))
    line = as_row(right, row)
    msg_ref[...] = jnp.broadcast_to(line.reshape(1, 1, 128), msg_ref.shape)


def near_first_kernel(in_ref, out_ref):
    sums = []
    for c in range(2):
        total = in_ref[8 * c]
        for y in range(1, 8):
            total = total + in_ref[8 * c + y]
        sums.append(total)
    right = sums[0] + sums[1]
    rows = jnp.where(lanes_of((1, 128)) < WIDE, pltpu.roll(sums[0], WIDE, 1), sums[1])
    both = jnp.concatenate([right, rows], axis=0)
    out_ref[...] = jnp.broadcast_to(both[None], out_ref.shape)


def near_next_kernel(in_ref, out_ref):
    total = in_ref[0]
    for i in range(1, in_ref.shape[0]):
        total = total + in_ref[i]
    out_ref[...] = jnp.broadcast_to(total[None], out_ref.shape)


def as_column(row, shape):
    on_diag = lanes_of(shape) == rows_of(shape)
    return jnp.sum(jnp.where(on_diag, row, 0.0), axis=1, keepdims=True)


def solved(gram, right):
    lanes, rows = lanes_of(gram.shape), rows_of(gram.shape)
    diag = (rows == lanes) & (rows < HIST)
    trace = jnp.sum(jnp.where(diag, gram, 0.0))
    a = gram + jnp.where(diag, RIDGE_SHARE * trace / HIST, 0.0)
    a = jnp.where(lanes == WIDE, as_column(right, gram.shape), a)
    for k in range(HIST):
        row = a[k : k + 1, :]
        row = row / row[:, k : k + 1]
        a = jnp.where(rows == k, row, a - a[:, k : k + 1] * row)
    return -jnp.broadcast_to(a[:, WIDE : WIDE + 1], a.shape)


def moved(image, coefficients, column):
    lines = [jnp.sum(coefficients * column(m), axis=0, keepdims=True) for m in range(PARTS)]
    return image + jnp.concatenate([*lines, jnp.zeros((16 - PARTS, 128), F32)], axis=0)


def chosen(x, qt):
    tall = jnp.concatenate(
        [jnp.zeros((WIDE, 128), F32), x, x, jnp.zeros((32, 128), F32)], axis=0
    )
    return dot(qt, tall.astype(BF16)).astype(BF16)


def far_first_kernel(in_ref, image_ref, wr_ref, qt_ref, send_ref, x_ref, gram_ref, gs):
    right = in_ref[0, 0:1, :]
    gs[0:1, :] = in_ref[0, 1:2, :]
    for i in range(1, 32):
        right = right + in_ref[i, 0:1, :]
        gs[i : i + 1, :] = in_ref[i, 1:2, :]
    half = gs[...]
    gram = jnp.concatenate([half, pltpu.roll(half, WIDE, 1)], axis=0)[:COLS]
    gram = jnp.where(lanes_of(gram.shape) < WIDE, gram, 0.0)
    gram_ref[...] = gram
    coefficients = solved(gram, right)
    x = moved(image_ref[...], coefficients, lambda m: wr_ref[m])
    x_ref[...] = x
    send_ref[...] = chosen(x, qt_ref[...]).astype(F32).reshape(send_ref.shape).astype(BF16)


def far_next_kernel(in_ref, gram_ref, image_ref, last_ref, wr_ref, qt_ref, send_ref, x_ref):
    total = in_ref[0]
    for i in range(1, 32):
        total = total + in_ref[i]
    gram = gram_ref[...]
    lanes, rows = lanes_of(gram.shape), rows_of(gram.shape)
    new_row = jnp.where(lanes_of(total.shape) < WIDE, pltpu.roll(total, WIDE, 1), 0.0)
    gram = jnp.where(rows == 0, new_row, gram)
    gram = jnp.where(lanes == 0, as_column(new_row, gram.shape), gram)
    coefficients = solved(gram, total)
    image = image_ref[...]
    step = image - last_ref[...]
    first = rows_of((COLS, 128)) == 0
    x = moved(image, coefficients, lambda m: jnp.where(first, step[m : m + 1, :], wr_ref[m]))
    for m in range(PARTS):
        x_ref[0, m // 3, m % 3 : m % 3 + 1, :] = x[m : m + 1, :]
    send_ref[...] = chosen(x, qt_ref[...]).astype(F32).reshape(send_ref.shape).astype(BF16)


def body(
    fluid_load,
    stiffness,
    mapping,
    live_count,
    dest_device,
    local_block,
    compliance,
    start_disp,
    residual_history,
    update_history,
):
    blocks = mapping.shape[0]
    sub_blocks = compliance.shape[1]
    peers = lax.axis_size(FLUID)
    near, far = lax.axis_size(NEAR), lax.axis_size(FAR)
    message = (peers, 8, 128)

    packed = jnp.swapaxes(start_disp[0].astype(BF16), 0, 1)
    whole = exchange(jnp.broadcast_to(packed, (peers, *packed.shape)), FLUID)

    dest = dest_device[:, 0]
    order = jnp.arange(blocks)
    earlier = (dest[:, None] == dest[None, :]) & (order[None, :] < order[:, None])
    slot = jnp.sum(earlier, axis=1)
    component = jnp.arange(8)
    column = dest[:, None] * 8 + slot[:, None] * 3 + component
    column = jnp.where(component < 3, column, -1).reshape(8 * blocks)
    whole_column = dest[:, None] * PARTS + component * sub_blocks + local_block[:, None]
    whole_column = jnp.where(component < 3, whole_column, -1).reshape(8 * blocks)
    pick = (column[:, None] == jnp.arange(8 * peers)[None, :]).astype(BF16)
    back = (jnp.arange(8 * peers)[:, None] == column[None, :]).astype(BF16)
    pick_whole = (whole_column[:, None] == jnp.arange(PARTS * peers)[None, :]).astype(BF16)
    alive = (order < live_count[0]).astype(F32)[:, None, None]
    load8 = jnp.pad(alive * fluid_load, ((0, 0), (0, 5), (0, 0))).reshape(8 * blocks, 128)
    stiff8 = jnp.pad(alive * stiffness, ((0, 0), (0, 5), (0, 0))).reshape(8 * blocks, 128)
    place = dest * 2 + slot
    names = jnp.sum(
        jnp.where(place[:, None] == jnp.arange(2 * peers)[None, :], local_block[:, None] + 1, 0), axis=0
    ).reshape(peers, 2, 1)
    part = jnp.arange(16)
    marks = ((names == part // 3 + 1) & (part < PARTS)).astype(F32).reshape(peers, 32)
    columns_first = lambda h: jnp.pad(
        jnp.moveaxis(h.reshape(HIST, PARTS, 128), 0, 1), ((0, 0), (0, COLS - HIST), (0, 0))
    )
    vr, wr = columns_first(residual_history), columns_first(update_history)
    basis = residual_history.reshape(HIST, -1)
    gram_local = jnp.pad(
        jnp.dot(basis, basis.T, precision=HIGHEST), ((0, peers - HIST), (0, WIDE - HIST))
    )
    gram_local = jnp.swapaxes(gram_local.reshape(2, far, WIDE), 0, 1).reshape(peers, WIDE)
    high, middle, low = three_pieces(gram_local)
    side = jnp.concatenate([high, middle, low, marks, jnp.zeros((peers, 32))], axis=1)
    side = jnp.pad(side.astype(BF16).reshape(peers, 2, 128), ((0, 0), (6, 0), (0, 0)))
    rows = lambda a: jnp.pad(a.reshape(PARTS, 128), ((0, 16 - PARTS), (0, 0)))
    comp, x = rows(compliance), rows(start_disp)

    square = pltpu.VMEM((8 * blocks, 128), F32)
    forces = lambda *args: call(
        forces_kernel, "forces", [(message, BF16)], *args, scratch=[square, square, square]
    )[0]
    sent = forces(whole.reshape(-1, 128), pick_whole, back, mapping, load8, stiff8, side)
    got = exchange(sent, FLUID)
    line, image, resid, q, qt = call(
        owner_first_kernel,
        "owner_first",
        [((near, 1, 128), F32), ((16, 128), F32), ((16, 128), F32), ((16, 8 * peers), BF16), ((8 * peers, 128), BF16)],
        got,
        comp,
        x,
        vr,
        scratch=[square],
    )
    line = exchange(line, NEAR)
    line = call(near_first_kernel, "near_first", [((far, 2, 128), F32)], line)[0]
    line = exchange(line, FAR)
    sent, x, gram = call(
        far_first_kernel,
        "far_first",
        [(message, BF16), ((16, 128), F32), ((COLS, 128), F32)],
        line,
        image,
        wr,
        qt,
        scratch=[pltpu.VMEM((far, 128), F32)],
    )

    got = exchange(sent, FLUID)
    sent = forces(got, pick, back, mapping, load8, stiff8, jnp.zeros_like(side))
    got = exchange(sent, FLUID)
    last_image = image
    line, image = call(
        owner_next_kernel,
        "owner_next",
        [((near, 1, 128), F32), ((16, 128), F32)],
        got,
        q,
        comp,
        x,
        resid,
        vr,
    )
    line = exchange(line, NEAR)
    line = call(near_next_kernel, "near_next", [((far, 1, 128), F32)], line)[0]
    line = exchange(line, FAR)
    sent, struct_disp = call(
        far_next_kernel,
        "far_next",
        [(message, BF16), (start_disp.shape, F32)],
        line,
        gram,
        image,
        last_image,
        wr,
        qt,
    )
    got = exchange(sent, FLUID)
    final_disp = call(
        final_kernel,
        "final",
        [(fluid_load.shape, F32)],
        live_count,
        got,
        pick,
        mapping,
        in_specs=[SMEM, VMEM, VMEM, VMEM],
        scratch=[square],
    )[0]
    return (struct_disp, final_disp)


def solution(mesh):
    split = Mesh(mesh.devices.reshape(8, 4, 2, mesh.shape["solid"]), ALL)
    in_specs = (
        P(ALL, None, None),
        P(ALL, None, None),
        P(ALL, None, None),
        P(ALL),
        P(ALL, None),
        P(ALL),
        P("solid", FLUID, None, None),
        P("solid", FLUID, None, None),
        P(None, "solid", FLUID, None, None),
        P(None, "solid", FLUID, None, None),
    )
    out_specs = (P("solid", FLUID, None, None), P(ALL, None, None))
    return jax.shard_map(body, mesh=split, in_specs=in_specs, out_specs=out_specs, check_vma=False)
```

time: 182 us -> 191 us (1.049)
  blocking collectives: 42.6 us -> 73.2 us
  Pallas kernels: 11.5 us -> 34.4 us
  waiting for transfers between devices: 52.2 us -> 29.6 us
  matrix products: 9.13 us -> 0.42 us
  starting transfers between devices: 38.9 us -> 32.3 us
  other arithmetic: 9.72 us -> 6.31 us
  local copies, waits for them, and re-layouts: 15.3 us -> 12.2 us
    all_to_all x3 -> x5, blocking collectives: 42.6 us -> 73.2 us  [exchange(): return lax.all_to_all(x, axes, split_axis=0, concat_axis=0, tiled=True)]
    pallas_call x2 -> x9, Pallas kernels: 11.5 us -> 34.4 us  [call(): pl.pallas_call(kernel, out_shape=[jax.ShapeDtypeStruct(shape, dtype) for...]
    all_to_all x6 -> x4, waiting for transfers between devices: 52.2 us -> 29.6 us  [exchange(): return lax.all_to_all(x, axes, split_axis=0, concat_axis=0, tiled=True)]
    dot_general x17 -> x1, matrix products: 9.13 us -> 0.42 us  [body(): jnp.dot(basis, basis.T, precision=HIGHEST)]
    all_to_all x6 -> x4, starting transfers between devices: 38.9 us -> 32.3 us  [exchange(): return lax.all_to_all(x, axes, split_axis=0, concat_axis=0, tiled=True)]
    another operation x6 -> x2, other arithmetic: 4.6 us -> 0.09 us
    unnamed x23 -> x28, local copies, waits for them, and re-layouts: 1.92 us -> 5.66 us
    scatter x3 -> x0, local copies, waits for them, and re-layouts: 3.69 us -> none  [the longest x2 3.68 us: solve_small(): system = system.at[:HIST, RHS].set(right_side)]
  transfers between devices with their start and end apart: 6 -> 4, of which waited for: 6 -> 4; matrix products, arithmetic and copies ran while one was open for 3% -> 7% of each run, Pallas kernels for 0% -> 0%
where the time goes in v2:
time: 191 us; the launch traced here: 190 us
  blocking collectives  73.2 us (38%)
  Pallas kernels  34.4 us (18%)
  starting transfers between devices  32.3 us (17%)
  waiting for transfers between devices  29.6 us (15%)
  local copies, waits for them, and re-layouts  12.2 us (6%)
  other arithmetic  6.31 us (3%)
    all_to_all x5, blocking collectives, exchange(): return lax.all_to_all(x, axes, split_axis=0, concat_axis=0, tiled=True)  73.2 us
    pallas_call x9, Pallas kernels, call(): pl.pallas_call(kernel, out_shape=[jax.ShapeDtypeStruct(shape, dtype) for...  34.4 us
    all_to_all x4, starting transfers between devices, exchange(): return lax.all_to_all(x, axes, split_axis=0, concat_axis=0, tiled=True)  32.3 us
    all_to_all x4, waiting for transfers between devices, exchange(): return lax.all_to_all(x, axes, split_axis=0, concat_axis=0, tiled=True)  29.6 us
    unnamed x28, local copies, waits for them, and re-layouts  5.66 us
  transfers between devices with their start and end apart: 4, of which 4 were waited for; matrix products, arithmetic and copies ran while one was open for 7% of the time, Pallas kernels for 0%

profile of v2, /device:TPU:1, one launch (start us, length us, event | category | flops | bytes accessed | tf_op | source)
XLA Modules:
  0.0 190.0 jit_solution(4922470210110068802)
XLA Ops:
  0.7 0.7 convert_bitcast_fusion
  2.1 14.8 %all-to-all-start = ((bf16[64,3,4,128]{3,2,1,0:T(4,128)(2,1)}), bf16[64,3,4,128]{3,2,1,0:T(4,128)(2,1)S(1)}, u32[]{:S(2)}, u32[]{:S(2)}) async-start(bf16[64,3,4,128]{3,2,1,0:T(4,128)(2,1)} %broadcast_in_dim.48), calls=%async_computation | async-start | bytes 393216 | tf_op jit(solution)/shard_map/all_to_all | solution.py:25
  17.0 0.9 convert_reduce_fusion
  19.3 0.7 add_select_fusion
  20.1 1.1 fusion.pick_ref
  24.2 0.8 pad_bitcast_fusion
  25.1 1.2 fusion.2
  26.3 2.7 %all-to-all-done = bf16[64,3,4,128]{3,2,1,0:T(4,128)(2,1)S(1)} async-done(((bf16[64,3,4,128]{3,2,1,0:T(4,128)(2,1)}), bf16[64,3,4,128]{3,2,1,0:T(4,128)(2,1)S(1)}, u32[]{:S(2)}, u32[]{:S(2)}) %all-to-all-start) | async-done | bytes 196640 | tf_op jit(solution)/shard_map/all_to_all | solution.py:25
  29.7 5.4 %forces.2 = bf16[64,8,128]{2,1,0:T(8,128)(2,1)} custom-call(bf16[768,128]{1,0:T(8,128)(2,1)} %bitcast.51, bf16[512,768]{1,0:T(8,128)(2,1)} %fusion.pick_ref, bf16[512,512]{1,0:T(8,128)(2,1)} %get-tuple-element.36.back_ref, bf16[64,128,128]{2,1,0:T(8,128)(2,1)} %map_ref.5, f32[512,128]{1,0:T(8,128)} %get-tuple-element.45.load_ref, ...), custom_call_target="tpu_custom_call" | custom-call | tf_op jit(solution)/shard_map/forces/pallas_call | solution.py:36
  35.1 7.7 %all-to-all-start.1 = ((bf16[64,8,128]{2,1,0:T(8,128)(2,1)}), bf16[64,8,128]{2,1,0:T(8,128)(2,1)S(1)}, u32[]{:S(2)}, u32[]{:S(2)}) async-start(bf16[64,8,128]{2,1,0:T(8,128)(2,1)} %forces.2), calls=%async_computation.1 | async-start | bytes 262144 | tf_op jit(solution)/shard_map/all_to_all | solution.py:25
  44.1 0.7 pad.35.vr_ref
  44.9 9.0 %all-to-all-done.1.got_ref = bf16[64,8,128]{2,1,0:T(8,128)(2,1)S(1)} async-done(((bf16[64,8,128]{2,1,0:T(8,128)(2,1)}), bf16[64,8,128]{2,1,0:T(8,128)(2,1)S(1)}, u32[]{:S(2)}, u32[]{:S(2)}) %all-to-all-start.1) | async-done | bytes 131104 | tf_op jit(solution)/shard_map/all_to_all | solution.py:25
  54.6 2.5 %owner_first.1 = (f32[16,1,128]{2,1,0:T(1,128)}, f32[16,128]{1,0:T(8,128)}, f32[16,128]{1,0:T(8,128)}, bf16[16,512]{1,0:T(8,128)(2,1)}, bf16[512,128]{1,0:T(8,128)(2,1)}) custom-call(bf16[64,8,128]{2,1,0:T(8,128)(2,1)} %copy-done.3, f32[16,128]{1,0:T(8,128)} %pad.33.comp_ref, f32[16,128]{1,0:T(8,128)} %pad.34.x_ref, f32[12,56,128]{2,1,0:T(8,128)} %pad.35.vr_ref), custom_call_target="tpu_custom_call" | custom-call | tf_op jit(solution)/shard_map/owner_first/pallas_call | solution.py:36
  57.0 14.4 %all_to_all.45.in_ref = f32[16,1,128]{2,1,0:T(1,128)} all-to-all(f32[16,1,128]{2,1,0:T(1,128)} %get-tuple-element.14), channel_id=1, replica_groups=mesh['z'=8,'x'=4,'c'=2,'solid'=8] {'c','solid'}, dimensions={0} | all-to-all | bytes 16384 | tf_op jit(solution)/shard_map/all_to_all | solution.py:25
  71.5 1.4 near_first.1
  72.9 3.9 %all-to-all-start.3 = ((f32[32,2,128]{2,1,0:T(2,128)}), f32[32,2,128]{2,1,0:T(2,128)S(1)}, u32[]{:S(2)}, u32[]{:S(2)}) async-start(f32[32,2,128]{2,1,0:T(2,128)} %near_first.1), calls=%async_computation.3 | async-start | bytes 65536 | tf_op jit(solution)/shard_map/all_to_all | solution.py:25
  76.8 0.8 pad.36.wr_ref
  77.6 7.8 %all-to-all-done.3.in_ref = f32[32,2,128]{2,1,0:T(2,128)S(1)} async-done(((f32[32,2,128]{2,1,0:T(2,128)}), f32[32,2,128]{2,1,0:T(2,128)S(1)}, u32[]{:S(2)}, u32[]{:S(2)}) %all-to-all-start.3) | async-done | bytes 32800 | tf_op jit(solution)/shard_map/all_to_all | solution.py:25
  86.0 6.4 %far_first.1 = (bf16[64,8,128]{2,1,0:T(8,128)(2,1)}, f32[16,128]{1,0:T(8,128)}, f32[56,128]{1,0:T(8,128)}) custom-call(f32[32,2,128]{2,1,0:T(2,128)} %copy-done.5, f32[16,128]{1,0:T(8,128)} %get-tuple-element.15.image_ref.last_ref, f32[12,56,128]{2,1,0:T(8,128)} %pad.36.wr_ref, bf16[512,128]{1,0:T(8,128)(2,1)} %get-tuple-element.16.qt_ref), custom_call_target="tpu_custom_call" | custom-call | tf_op jit(solution)/shard_map/far_first/pallas_call | solution.py:36
  92.4 18.0 %all_to_all.46.x_ref = bf16[64,8,128]{2,1,0:T(8,128)(2,1)} all-to-all(bf16[64,8,128]{2,1,0:T(8,128)(2,1)} %get-tuple-element.17), channel_id=1, replica_groups=mesh['z'=8,'x'=4,'c'=2,'solid'=8] {'z','x','c'}, dimensions={0} | all-to-all | bytes 262144 | tf_op jit(solution)/shard_map/all_to_all | solution.py:25
  111.1 5.1 %forces.3 = bf16[64,8,128]{2,1,0:T(8,128)(2,1)} custom-call(bf16[64,8,128]{2,1,0:T(8,128)(2,1)} %all_to_all.46.x_ref, bf16[512,512]{1,0:T(8,128)(2,1)} %get-tuple-element.35.pick_ref, bf16[512,512]{1,0:T(8,128)(2,1)} %get-tuple-element.36.back_ref, bf16[64,128,128]{2,1,0:T(8,128)(2,1)} %map_ref.5, f32[512,128]{1,0:T(8,128)} %get-tuple-element.45.load_ref, ...), custom_call_target="tpu_custom_call" | custom-call | tf_op jit(solution)/shard_map/forces/pallas_call | solution.py:36
  116.2 16.5 %all_to_all.47.got_ref = bf16[64,8,128]{2,1,0:T(8,128)(2,1)} all-to-all(bf16[64,8,128]{2,1,0:T(8,128)(2,1)} %forces.3), channel_id=1, replica_groups=mesh['z'=8,'x'=4,'c'=2,'solid'=8] {'z','x','c'}, dimensions={0} | all-to-all | bytes 262144 | tf_op jit(solution)/shard_map/all_to_all | solution.py:25
  132.7 2.1 %owner_next.1 = (f32[16,1,128]{2,1,0:T(1,128)}, f32[16,128]{1,0:T(8,128)}) custom-call(bf16[64,8,128]{2,1,0:T(8,128)(2,1)} %all_to_all.47.got_ref, bf16[16,512]{1,0:T(8,128)(2,1)} %get-tuple-element.18.q_ref, f32[16,128]{1,0:T(8,128)} %pad.33.comp_ref, f32[16,128]{1,0:T(8,128)} %get-tuple-element.19.x_ref, f32[16,128]{1,0:T(8,128)} %get-tuple-element.20.last_ref, ...), custom_call_target="tpu_custom_call" | custom-call | tf_op jit(solution)/shard_map/owner_next/pallas_call | solution.py:36
  134.8 11.3 %all_to_all.48.in_ref = f32[16,1,128]{2,1,0:T(1,128)} all-to-all(f32[16,1,128]{2,1,0:T(1,128)} %get-tuple-element.21), channel_id=1, replica_groups=mesh['z'=8,'x'=4,'c'=2,'solid'=8] {'c','solid'}, dimensions={0} | all-to-all | bytes 16384 | tf_op jit(solution)/shard_map/all_to_all | solution.py:25
  146.0 1.3 near_next.1
  147.4 13.0 %all_to_all.49.in_ref = f32[32,1,128]{2,1,0:T(1,128)} all-to-all(f32[32,1,128]{2,1,0:T(1,128)} %near_next.1), channel_id=1, replica_groups=mesh['z'=8,'x'=4,'c'=2,'solid'=8] {'z','x'}, dimensions={0} | all-to-all | bytes 32768 | tf_op jit(solution)/shard_map/all_to_all | solution.py:25
  160.4 6.6 %far_next.1 = (bf16[64,8,128]{2,1,0:T(8,128)(2,1)}, f32[1,4,3,128]{3,2,1,0:T(4,128)}) custom-call(f32[32,1,128]{2,1,0:T(1,128)} %all_to_all.49.in_ref, f32[56,128]{1,0:T(8,128)} %get-tuple-element.22.gram_ref, f32[16,128]{1,0:T(8,128)} %get-tuple-element.23.image_ref, f32[16,128]{1,0:T(8,128)} %get-tuple-element.15.image_ref.last_ref, ...), custom_call_target="tpu_custom_call" | custom-call | tf_op jit(solution)/shard_map/far_next/pallas_call | solution.py:36
  167.0 5.9 %all-to-all-start.8 = ((bf16[64,8,128]{2,1,0:T(8,128)(2,1)}), bf16[64,8,128]{2,1,0:T(8,128)(2,1)S(1)}, u32[]{:S(2)}, u32[]{:S(2)}) async-start(bf16[64,8,128]{2,1,0:T(8,128)(2,1)} %get-tuple-element.25), calls=%async_computation.8 | async-start | bytes 262144 | tf_op jit(solution)/shard_map/all_to_all | solution.py:25
  172.9 1.3 copy.47
  174.2 10.0 %all-to-all-done.8.x_ref = bf16[64,8,128]{2,1,0:T(8,128)(2,1)S(1)} async-done(((bf16[64,8,128]{2,1,0:T(8,128)(2,1)}), bf16[64,8,128]{2,1,0:T(8,128)(2,1)S(1)}, u32[]{:S(2)}, u32[]{:S(2)}) %all-to-all-start.8) | async-done | bytes 131104 | tf_op jit(solution)/shard_map/all_to_all | solution.py:25
  184.9 3.5 %final.1 = f32[64,3,128]{2,1,0:T(4,128)} custom-call(s32[1]{0:T(128)} %copy.54.live_ref, bf16[64,8,128]{2,1,0:T(8,128)(2,1)} %copy-done.2, bf16[512,512]{1,0:T(8,128)(2,1)} %get-tuple-element.35.pick_ref, bf16[64,128,128]{2,1,0:T(8,128)(2,1)} %map_ref.5), custom_call_target="tpu_custom_call" | custom-call | tf_op jit(solution)/shard_map/final/pallas_call | solution.py:36
  188.4 1.6 copy.48
  (59 shorter events, 9.0 us)
Async XLA Ops:
  0.6 21.2 %copy-start = (f32[50,1,4,3,128]{4,2,3,1,0:T(4,128)S(1)}, f32[50,1,4,3,128]{4,2,3,1,0:T(4,128)}, u32[]{:S(2)}) copy-start(f32[50,1,4,3,128]{4,2,3,1,0:T(4,128)} %param.18) | copy-start | bytes 921604
  0.6 21.8 %copy-start.6 = (f32[64,3,128]{2,0,1:T(8,128)S(1)}, f32[64,3,128]{2,0,1:T(8,128)}, u32[]{:S(2)}) copy-start(f32[64,3,128]{2,0,1:T(8,128)} %param.11) | copy-start | bytes 294916
  0.6 21.8 %copy-start.7 = (f32[64,3,128]{2,0,1:T(8,128)S(1)}, f32[64,3,128]{2,0,1:T(8,128)}, u32[]{:S(2)}) copy-start(f32[64,3,128]{2,0,1:T(8,128)} %param.10) | copy-start | bytes 294916
  2.1 26.8 %all-to-all-start = ((bf16[64,3,4,128]{3,2,1,0:T(4,128)(2,1)}), bf16[64,3,4,128]{3,2,1,0:T(4,128)(2,1)S(1)}, u32[]{:S(2)}, u32[]{:S(2)}) async-start(bf16[64,3,4,128]{3,2,1,0:T(4,128)(2,1)} %broadcast_in_dim.48), calls=%async_computation | async-start | bytes 393216 | tf_op jit(solution)/shard_map/all_to_all | solution.py:25
  29.0 0.7 copy-start.1
  29.7 13.2 %copy-start.8 = (f32[1,4,3,128]{3,1,2,0:T(4,128)S(1)}, f32[1,4,3,128]{3,1,2,0:T(4,128)}, u32[]{:S(2)}) copy-start(f32[1,4,3,128]{3,1,2,0:T(4,128)} %param.17) | copy-start | bytes 18436
  29.7 13.2 %copy-start.9 = (f32[1,4,3,128]{3,1,2,0:T(4,128)S(1)}, f32[1,4,3,128]{3,1,2,0:T(4,128)}, u32[]{:S(2)}) copy-start(f32[1,4,3,128]{3,1,2,0:T(4,128)} %param.16) | copy-start | bytes 18436
  35.1 41.6 %copy-start.4 = (f32[50,1,4,3,128]{4,2,3,1,0:T(4,128)S(1)}, f32[50,1,4,3,128]{4,2,3,1,0:T(4,128)}, u32[]{:S(2)}) copy-start(f32[50,1,4,3,128]{4,2,3,1,0:T(4,128)} %param.19) | copy-start | bytes 921604
  35.1 18.8 %all-to-all-start.1 = ((bf16[64,8,128]{2,1,0:T(8,128)(2,1)}), bf16[64,8,128]{2,1,0:T(8,128)(2,1)S(1)}, u32[]{:S(2)}, u32[]{:S(2)}) async-start(bf16[64,8,128]{2,1,0:T(8,128)(2,1)} %forces.2), calls=%async_computation.1 | async-start | bytes 262144 | tf_op jit(solution)/shard_map/all_to_all | solution.py:25
  53.9 0.6 copy-start.3
  72.9 12.5 %all-to-all-start.3 = ((f32[32,2,128]{2,1,0:T(2,128)}), f32[32,2,128]{2,1,0:T(2,128)S(1)}, u32[]{:S(2)}, u32[]{:S(2)}) async-start(f32[32,2,128]{2,1,0:T(2,128)} %near_first.1), calls=%async_computation.3 | async-start | bytes 65536 | tf_op jit(solution)/shard_map/all_to_all | solution.py:25
  85.4 0.6 copy-start.5
  167.0 17.2 %all-to-all-start.8 = ((bf16[64,8,128]{2,1,0:T(8,128)(2,1)}), bf16[64,8,128]{2,1,0:T(8,128)(2,1)S(1)}, u32[]{:S(2)}, u32[]{:S(2)}) async-start(bf16[64,8,128]{2,1,0:T(8,128)(2,1)} %get-tuple-element.25), calls=%async_computation.8 | async-start | bytes 262144 | tf_op jit(solution)/shard_map/all_to_all | solution.py:25
  184.2 0.6 copy-start.2

commit v3 on v2

v3 whole, which is shorter than its diff:
```python
import jax
import jax.numpy as jnp
from jax import lax
from jax.experimental import pallas as pl
from jax.experimental.pallas import tpu as pltpu
from jax.sharding import Mesh
from jax.sharding import PartitionSpec as P

HIST = 50
RIDGE_SHARE = 0.01
ALL = ("z", "x", "c", "solid")
FLUID = ("z", "x", "c")
NEAR = ("c", "solid")
FAR = ("z", "x")
COLS = 56
PARTS = 12
WIDE = 64
F32, BF16 = jnp.float32, jnp.bfloat16
HIGHEST = lax.Precision.HIGHEST
VMEM = pl.BlockSpec(memory_space=pltpu.VMEM)
SMEM = pl.BlockSpec(memory_space=pltpu.SMEM)


def exchange(x, axes):
    return lax.all_to_all(x, axes, split_axis=0, concat_axis=0, tiled=True)


def call(kernel, name, outs, *args, in_specs=None, scratch=(), mib=2, cost=None):
    return pl.pallas_call(
        kernel,
        out_shape=[jax.ShapeDtypeStruct(shape, dtype) for shape, dtype in outs],
        compiler_params=pltpu.CompilerParams(vmem_limit_bytes=mib << 20),
        in_specs=in_specs or [VMEM] * len(args),
        out_specs=[VMEM] * len(outs),
        scratch_shapes=list(scratch),
        cost_estimate=cost,
        name=name,
    )(*args)


def dot(a, b, dims=((1,), (0,)), precision=None):
    return lax.dot_general(a, b, (dims, ((), ())), precision=precision, preferred_element_type=F32)


def lanes_of(shape):
    return lax.broadcasted_iota(jnp.int32, shape, len(shape) - 1)


def rows_of(shape):
    return lax.broadcasted_iota(jnp.int32, shape, 0)


def every(ref, part):
    return ref[pl.ds(part, HIST, stride=PARTS), :]


def as_column(row, shape):
    on_diag = lanes_of(shape) == rows_of(shape)
    return jnp.sum(jnp.where(on_diag, row, jnp.zeros_like(row)), axis=1, keepdims=True)


def spread_kernel(live_ref, x_ref, out_ref, alive_ref):
    alive_ref[...] = jnp.where(rows_of(alive_ref.shape) < live_ref[0], 1.0, 0.0)
    out_ref[...] = jnp.broadcast_to(x_ref[...].astype(BF16)[None], out_ref.shape)


def forces_first_kernel(
    alive_ref, x_ref, dest_ref, local_ref, hist_ref, raw_load_ref, raw_stiff_ref, map_ref, comp_ref, start_ref,
    out_ref, pick_ref, back_ref, load_ref, stiff_ref, flat_comp_ref, flat_start_ref, gs, ss, whole_ref, xs, us,
):
    for c in range(3):
        flat_comp_ref[4 * c : 4 * c + 4, :] = comp_ref[c]
        flat_start_ref[4 * c : 4 * c + 4, :] = start_ref[c]
    square = (64, 128)
    lanes, rows = lanes_of(square), rows_of(square)
    dest = jnp.where(lanes < 64, jnp.concatenate([dest_ref[...]] * 2, axis=1), -1)
    local = jnp.concatenate([local_ref[...]] * 2, axis=1)
    dest_column = as_column(dest.astype(F32), square)
    local_column = as_column(local.astype(F32), square).astype(jnp.int32)
    same = (dest_column == dest.astype(F32)) & (lanes < 64)
    dest_column = dest_column.astype(jnp.int32)
    slot_column = jnp.sum(jnp.where(same & (lanes < rows), 1.0, 0.0), axis=1, keepdims=True)
    slot_row = jnp.sum(jnp.where(same & (rows < lanes), 1.0, 0.0), axis=0, keepdims=True)
    slot_column = slot_column.astype(jnp.int32)
    place_column = dest_column * 8 + slot_column * 4
    place_row = dest[0:1] * 8 + slot_row.astype(jnp.int32) * 4
    wide = lanes_of((64, 512))
    wider = lanes_of((64, 768))
    for c in range(3):
        pick_ref[64 * c : 64 * c + 64, :] = jnp.where(wide == place_column + c, 1.0, 0.0).astype(BF16)
        whole_column = dest_column * PARTS + 4 * c + local_column
        whole_ref[64 * c : 64 * c + 64, :] = jnp.where(wider == whole_column, 1.0, 0.0).astype(BF16)
    tall = rows_of((512, 128))
    low = lanes[0:1] < 64
    first = jnp.where(low, place_row, pltpu.roll(place_row, 64, 1) + 1)
    second = jnp.where(low, place_row + 2, -1)
    back_ref[:, 0:128] = jnp.where(tall == first, 1.0, 0.0).astype(BF16)
    back_ref[:, 128:256] = jnp.where(tall == second, 1.0, 0.0).astype(BF16)
    part = lanes % 16
    held = (lanes >= 64) & (lanes // 16 - 4 == slot_column) & (part % 4 == local_column) & (part < PARTS)
    onto = jnp.where(dest == rows, 1.0, 0.0).astype(BF16)
    marks = dot(onto[:, 0:64], jnp.where(held, 1.0, 0.0).astype(BF16))
    history = jnp.concatenate([every(hist_ref, m) for m in range(PARTS)], axis=1)
    gs[...] = jnp.zeros(square, F32)
    gs[0:HIST, 0:HIST] = dot(history, history, ((1,), (1,)), HIGHEST)
    gram = gs[...]
    high = gram.astype(BF16).astype(F32)
    middle = (gram - high).astype(BF16).astype(F32)
    low_part = gram - high - middle
    ss[...] = jnp.zeros((512, 128), F32)
    ss[pl.ds(3, 64, stride=8), :] = high + pltpu.roll(middle, WIDE, 1)
    ss[pl.ds(7, 64, stride=8), :] = low_part + marks
    alive = alive_ref[...]
    for c in range(3):
        load_ref[64 * c : 64 * c + 64, :] = raw_load_ref[64 * c : 64 * c + 64, :] * alive
        stiff_ref[64 * c : 64 * c + 64, :] = raw_stiff_ref[64 * c : 64 * c + 64, :] * alive
    filled = forces(x_ref, whole_ref, back_ref, map_ref, load_ref, stiff_ref, xs, us)
    out_ref[...] = (filled + ss[...]).astype(BF16)


def apply_maps(map_ref, from_ref, to_ref, dims):
    for b in range(map_ref.shape[0]):
        rows = pl.ds(b, 3, stride=64)
        to_ref[rows, :] = dot(from_ref[rows, :].astype(BF16), map_ref[b], dims)


def forces(x_ref, pick_ref, back_ref, map_ref, load_ref, stiff_ref, xs, us):
    xs[...] = dot(pick_ref[...], x_ref[...])
    apply_maps(map_ref, xs, us, ((1,), (0,)))
    xs[...] = load_ref[...] - stiff_ref[...] * us[...]
    apply_maps(map_ref, xs, us, ((1,), (1,)))
    contrib = jnp.concatenate([us[...].astype(BF16), jnp.zeros((64, 128), BF16)], axis=0)
    return dot(back_ref[...], contrib)


def forces_next_kernel(x_ref, pick_ref, back_ref, map_ref, load_ref, stiff_ref, out_ref, xs, us):
    out_ref[...] = forces(x_ref, pick_ref, back_ref, map_ref, load_ref, stiff_ref, xs, us).astype(BF16)


def final_kernel(x_ref, pick_ref, map_ref, alive_ref, struct_ref, out_ref, disp_ref, xs, us):
    for c in range(3):
        disp_ref[c] = struct_ref[4 * c : 4 * c + 4, :]
    xs[...] = dot(pick_ref[...], x_ref[...])
    apply_maps(map_ref, xs, us, ((1,), (0,)))
    for c in range(3):
        out_ref[64 * c : 64 * c + 64, :] = us[64 * c : 64 * c + 64, :] * alive_ref[...]


def history_sums(hist_ref, vector):
    acc = every(hist_ref, 0) * vector[0:1, :]
    for m in range(1, PARTS):
        acc = acc + every(hist_ref, m) * vector[m : m + 1, :]
    return acc


def as_row(scratch, first, second):
    scratch[...] = jnp.zeros(scratch.shape, F32)
    scratch[0:HIST, :] = first
    if second is not None:
        scratch[WIDE : WIDE + HIST, :] = second
    return dot(jnp.ones((8, 128), F32), scratch[...], ((1,), (1,)), HIGHEST)[0:1, :]


def owner_first_kernel(got_ref, comp_ref, x_ref, hist_ref, msg_ref, image_ref, resid_ref, q_ref, qt_ref, xs, hs):
    got = got_ref[...]
    xs[...] = got.astype(F32)
    mark3 = xs[pl.ds(3, 64, stride=8), :]
    mark7 = xs[pl.ds(7, 64, stride=8), :]
    sum3 = jnp.sum(mark3, axis=0, keepdims=True)
    sum7 = jnp.sum(mark7, axis=0, keepdims=True)
    gram_row = sum3 + pltpu.roll(sum3, WIDE, 1) + pltpu.roll(sum7, WIDE, 1)
    spread = jnp.where(lanes_of((64, 512)) // 8 == rows_of((64, 512)), 1.0, 0.0).astype(BF16)
    wide = dot(mark7.astype(BF16), spread, ((0,), (0,)))
    part = rows_of((16, 512))
    row = lanes_of((16, 512)) % 8
    match = (part // 4 == row % 4) & (part < PARTS)
    q = jnp.where(match & (row < 4), wide[64:80], 0.0)
    q = (q + jnp.where(match & (row >= 4), wide[80:96], 0.0)).astype(BF16)
    q_ref[...] = q
    tall = jnp.broadcast_to(xs[...].reshape(64, 8, 128)[:, 7:8, :], (64, 8, 128)).reshape(512, 128)
    lane = lanes_of((512, 128))
    row = rows_of((512, 128)) % 8
    match = ((lane % 16) // 4 == row % 4) & (lane // 16 - 4 == row // 4) & (lane % 16 < PARTS)
    qt_ref[...] = jnp.where(match, tall, 0.0).astype(BF16)
    image = comp_ref[...] * dot(q, got)[0:PARTS]
    resid = image - x_ref[...]
    image_ref[...] = image
    resid_ref[...] = resid
    line = as_row(hs, history_sums(hist_ref, resid), None)
    line = jnp.where(lanes_of(line.shape) < WIDE, line, gram_row)
    msg_ref[...] = jnp.broadcast_to(line.reshape(1, 1, 128), msg_ref.shape)


def owner_next_kernel(got_ref, q_ref, comp_ref, x_ref, last_ref, hist_ref, msg_ref, image_ref, hs):
    image = comp_ref[...] * dot(q_ref[...], got_ref[...])[0:PARTS]
    image_ref[...] = image
    resid = image - x_ref[...]
    newest = resid - last_ref[...]
    first = rows_of((HIST, 128)) == 0
    own_right = jnp.sum(newest * resid, axis=0, keepdims=True)
    own_row = jnp.sum(newest * newest, axis=0, keepdims=True)
    right = jnp.where(first, own_right, history_sums(hist_ref, resid))
    row = jnp.where(first, own_row, history_sums(hist_ref, newest))
    line = as_row(hs, right, row)
    msg_ref[...] = jnp.broadcast_to(line.reshape(1, 1, 128), msg_ref.shape)


def near_first_kernel(in_ref, out_ref):
    sums = []
    for c in range(2):
        total = in_ref[8 * c]
        for y in range(1, 8):
            total = total + in_ref[8 * c + y]
        sums.append(total)
    right = sums[0] + sums[1]
    rows = jnp.where(lanes_of((1, 128)) < WIDE, pltpu.roll(sums[0], WIDE, 1), sums[1])
    both = jnp.concatenate([right, rows], axis=0)
    out_ref[...] = jnp.broadcast_to(both[None], out_ref.shape)


def near_next_kernel(in_ref, out_ref):
    total = in_ref[0]
    for i in range(1, in_ref.shape[0]):
        total = total + in_ref[i]
    out_ref[...] = jnp.broadcast_to(total[None], out_ref.shape)


def solved(gram, right):
    lanes, rows = lanes_of(gram.shape), rows_of(gram.shape)
    diag = (rows == lanes) & (rows < HIST)
    trace = jnp.sum(jnp.sum(jnp.where(diag, gram, 0.0), axis=1, keepdims=True), axis=0, keepdims=True)
    scale = 1.0 / trace
    a = gram * scale + jnp.where(diag, RIDGE_SHARE / HIST, 0.0)
    a = jnp.where(lanes == WIDE, as_column(right * scale, gram.shape), a)
    tiles = [a[8 * i : 8 * i + 8] for i in range(COLS // 8)]
    sub = rows_of((8, 128))
    for k in range(0, HIST, 2):
        t, s = k // 8, k % 8
        lefts = [jnp.broadcast_to(tile[:, k : k + 1], (8, 128)) for tile in tiles]
        rights = [jnp.broadcast_to(tile[:, k + 1 : k + 2], (8, 128)) for tile in tiles]
        p11, p12 = lefts[t][s : s + 1], rights[t][s : s + 1]
        p21, p22 = lefts[t][s + 1 : s + 2], rights[t][s + 1 : s + 2]
        row1, row2 = tiles[t][s : s + 1], tiles[t][s + 1 : s + 2]
        inverse = 1.0 / (p11 * p22 - p12 * p21)
        new1 = (p22 * row1 - p12 * row2) * inverse
        new2 = (p11 * row2 - p21 * row1) * inverse
        tiles = [tile - left * new1 - right * new2 for tile, left, right in zip(tiles, lefts, rights)]
        tiles[t] = jnp.where(sub == s, new1, jnp.where(sub == s + 1, new2, tiles[t]))
    a = jnp.concatenate(tiles, axis=0)
    return -jnp.broadcast_to(a[:, WIDE : WIDE + 1], a.shape)[:HIST]


def moved(image, coefficients, column):
    lines = [jnp.sum(coefficients * column(m), axis=0, keepdims=True) for m in range(PARTS)]
    return image + jnp.concatenate(lines, axis=0)


def chosen(x, qt, xs):
    xs[...] = jnp.zeros(xs.shape, F32)
    xs[WIDE : WIDE + PARTS, :] = x
    xs[WIDE + 16 : WIDE + 16 + PARTS, :] = x
    return dot(qt, xs[...].astype(BF16)).astype(BF16)


def far_first_kernel(in_ref, image_ref, upd_ref, qt_ref, send_ref, x_ref, gram_ref, hs, gs, xs):
    right = in_ref[0, 0:1, :]
    hs[0:1, :] = in_ref[0, 1:2, :]
    for i in range(1, 32):
        right = right + in_ref[i, 0:1, :]
        hs[i : i + 1, :] = in_ref[i, 1:2, :]
    half = hs[...]
    gs[pl.ds(0, 32, stride=2), :] = half
    gs[pl.ds(1, 32, stride=2), :] = pltpu.roll(half, WIDE, 1)
    gram = gs[0:COLS, :]
    gram = jnp.where(lanes_of(gram.shape) < WIDE, gram, 0.0)
    gram_ref[...] = gram
    coefficients = solved(gram, right)
    x = moved(image_ref[...], coefficients, lambda m: every(upd_ref, m))
    x_ref[...] = x
    send_ref[...] = chosen(x, qt_ref[...], xs)


def far_next_kernel(in_ref, gram_ref, image_ref, last_ref, upd_ref, qt_ref, send_ref, x_ref, xs):
    total = in_ref[0]
    for i in range(1, 32):
        total = total + in_ref[i]
    gram = gram_ref[...]
    lanes, rows = lanes_of(gram.shape), rows_of(gram.shape)
    new_row = jnp.where(lanes_of(total.shape) < WIDE, pltpu.roll(total, WIDE, 1), 0.0)
    gram = jnp.where(rows == 0, new_row, gram)
    gram = jnp.where(lanes == 0, as_column(new_row, gram.shape), gram)
    coefficients = solved(gram, total)
    image = image_ref[...]
    step = image - last_ref[...]
    first = rows_of((HIST, 128)) == 0
    x = moved(image, coefficients, lambda m: jnp.where(first, step[m : m + 1, :], every(upd_ref, m)))
    x_ref[...] = x
    send_ref[...] = chosen(x, qt_ref[...], xs)


def body(
    fluid_load,
    stiffness,
    mapping,
    live_count,
    dest_device,
    local_block,
    compliance,
    start_disp,
    residual_history,
    update_history,
):
    blocks = mapping.shape[0]
    peers = lax.axis_size(FLUID)
    near, far = lax.axis_size(NEAR), lax.axis_size(FAR)
    rows = 8 * peers
    over_fluid = lambda x: exchange(x.reshape(peers, 8, 128), FLUID).reshape(rows, 128)
    parts = lambda a: jnp.swapaxes(a, -3, -2)
    history, updates = (parts(a).reshape(-1, 128) for a in (residual_history, update_history))
    by_part = lambda a: jnp.swapaxes(a, 0, 1).reshape(3 * blocks, 128)
    start = parts(start_disp)[0]
    lines = pltpu.VMEM((3 * blocks, 128), F32)
    square = pltpu.VMEM((128, 128), F32)
    tall = pltpu.VMEM((rows, 128), F32)

    whole, alive = call(
        spread_kernel,
        "spread",
        [((peers, 3, 4, 128), BF16), ((blocks, 128), F32)],
        live_count,
        start,
        in_specs=[SMEM, VMEM],
        cost=pl.CostEstimate(flops=20_000_000_000, bytes_accessed=50_000_000, transcendentals=0),
    )
    whole = exchange(whole, FLUID).reshape(PARTS * peers, 128)
    sent, pick, back, load, stiff, comp, start = call(
        forces_first_kernel,
        "forces_first",
        [
            ((rows, 128), BF16),
            ((3 * blocks, rows), BF16),
            ((rows, 256), BF16),
            ((3 * blocks, 128), F32),
            ((3 * blocks, 128), F32),
            ((PARTS, 128), F32),
            ((PARTS, 128), F32),
        ],
        alive,
        whole,
        dest_device.reshape(1, blocks),
        local_block.reshape(1, blocks),
        history,
        by_part(fluid_load),
        by_part(stiffness),
        mapping,
        parts(compliance)[0],
        start,
        scratch=[
            pltpu.VMEM((64, 128), F32),
            tall,
            pltpu.VMEM((3 * blocks, PARTS * peers), BF16),
            lines,
            lines,
        ],
        mib=8,
    )
    got = over_fluid(sent)
    line, image, resid, q, qt = call(
        owner_first_kernel,
        "owner_first",
        [((near, 1, 128), F32), ((PARTS, 128), F32), ((PARTS, 128), F32), ((16, rows), BF16), ((rows, 128), BF16)],
        got,
        comp,
        start,
        history,
        scratch=[tall, square],
        mib=4,
    )
    line = exchange(line, NEAR)
    line = call(near_first_kernel, "near_first", [((far, 2, 128), F32)], line)[0]
    line = exchange(line, FAR)
    sent, x, gram = call(
        far_first_kernel,
        "far_first",
        [((rows, 128), BF16), ((PARTS, 128), F32), ((COLS, 128), F32)],
        line,
        image,
        updates,
        qt,
        scratch=[pltpu.VMEM((far, 128), F32), pltpu.VMEM((64, 128), F32), square],
    )
    got = over_fluid(sent)
    sent = call(
        forces_next_kernel,
        "forces_next",
        [((rows, 128), BF16)],
        got,
        pick,
        back,
        mapping,
        load,
        stiff,
        scratch=[lines, lines],
        mib=6,
    )[0]
    got = over_fluid(sent)
    last_image = image
    line, image = call(
        owner_next_kernel,
        "owner_next",
        [((near, 1, 128), F32), ((PARTS, 128), F32)],
        got,
        q,
        comp,
        x,
        resid,
        history,
        scratch=[square],
    )
    line = exchange(line, NEAR)
    line = call(near_next_kernel, "near_next", [((far, 1, 128), F32)], line)[0]
    line = exchange(line, FAR)
    sent, struct_disp = call(
        far_next_kernel,
        "far_next",
        [((rows, 128), BF16), ((PARTS, 128), F32)],
        line,
        gram,
        image,
        last_image,
        updates,
        qt,
        scratch=[square],
    )
    got = over_fluid(sent)
    final_disp, struct_disp = call(
        final_kernel,
        "final",
        [((3 * blocks, 128), F32), ((3, 4, 128), F32)],
        got,
        pick,
        mapping,
        alive,
        struct_disp,
        scratch=[lines, lines],
        mib=6,
    )
    struct_disp = parts(struct_disp[None])
    return (struct_disp, jnp.swapaxes(final_disp.reshape(3, blocks, 128), 0, 1))


def solution(mesh):
    split = Mesh(mesh.devices.reshape(8, 4, 2, mesh.shape["solid"]), ALL)
    in_specs = (
        P(ALL, None, None),
        P(ALL, None, None),
        P(ALL, None, None),
        P(ALL),
        P(ALL, None),
        P(ALL),
        P("solid", FLUID, None, None),
        P("solid", FLUID, None, None),
        P(None, "solid", FLUID, None, None),
        P(None, "solid", FLUID, None, None),
    )
    out_specs = (P("solid", FLUID, None, None), P(ALL, None, None))
    return jax.shard_map(body, mesh=split, in_specs=in_specs, out_specs=out_specs, check_vma=False)
```

time: 191 us -> 154 us (0.81)
  blocking collectives: 73.2 us -> 138 us
  starting transfers between devices: 32.3 us -> 0 us
  waiting for transfers between devices: 29.6 us -> 0 us
  Pallas kernels: 34.4 us -> 13.8 us
  local copies, waits for them, and re-layouts: 12.2 us -> 0.72 us
  other arithmetic: 6.31 us -> 0 us
    all_to_all x5 -> x9, blocking collectives: 73.2 us -> 138 us  [exchange(): return lax.all_to_all(x, axes, split_axis=0, concat_axis=0, tiled=True)]
    all_to_all x4 -> x0, starting transfers between devices: 32.3 us -> none  [exchange(): return lax.all_to_all(x, axes, split_axis=0, concat_axis=0, tiled=True)]
    all_to_all x4 -> x0, waiting for transfers between devices: 29.6 us -> none  [exchange(): return lax.all_to_all(x, axes, split_axis=0, concat_axis=0, tiled=True)]
    pallas_call x9 -> x10, Pallas kernels: 34.4 us -> 13.8 us  [call(): pl.pallas_call(kernel, out_shape=[jax.ShapeDtypeStruct(shape, dtype) for...]
    unnamed x28 -> x20, local copies, waits for them, and re-layouts: 5.66 us -> 0.72 us
    pad x6 -> x0, local copies, waits for them, and re-layouts: 3.42 us -> none  [the longest x2 1.51 us: body(): jnp.pad(jnp.moveaxis(h.reshape(HIST, PARTS, 128), 0, 1), ((0, 0), (0, COL...]
    convert_element_type x3 -> x0, other arithmetic: 2.29 us -> none  [the longest x1 1.19 us: body(): pick = (column[:, None] == jnp.arange(8 * peers)[None, :]).astype(BF16)]
  transfers between devices with their start and end apart: 4 -> 0, of which waited for: 4 -> 0; matrix products, arithmetic and copies ran while one was open for 7% -> 0% of each run, Pallas kernels for 0% -> 0%
where the time goes in v3:
time: 154 us
  blocking collectives  138 us (90%)
  Pallas kernels  13.8 us (9%)
    all_to_all x9, blocking collectives, exchange(): return lax.all_to_all(x, axes, split_axis=0, concat_axis=0, tiled=True)  138 us
    pallas_call x10, Pallas kernels, call(): pl.pallas_call(kernel, out_shape=[jax.ShapeDtypeStruct(shape, dtype) for...  13.8 us

profile of v3, /device:TPU:1, one launch (start us, length us, event | category | flops | bytes accessed | tf_op | source)
XLA Modules:
  0.0 153.8 jit_solution(17162587537871296322)
XLA Ops:
  1.3 0.0 copy-start.5
  1.3 0.7 copy-done.5
  2.0 0.0 copy-start.6
  2.0 0.0 copy-start.7
  2.0 0.0 copy-start.8
  2.0 0.0 copy-start.9
  2.0 0.1 spread.1
  2.1 0.0 copy-start.2
  2.1 26.9 %all_to_all.45 = bf16[64,3,4,128]{3,2,1,0:T(4,128)(2,1)S(1)} all-to-all(bf16[64,3,4,128]{3,2,1,0:T(4,128)(2,1)S(1)} %get-tuple-element.26), channel_id=1, replica_groups=mesh['z'=8,'x'=4,'c'=2,'solid'=8] {'z','x','c'}, dimensions={0} | all-to-all | bytes 393216 | tf_op jit(solution)/shard_map/all_to_all | solution.py:25
  29.0 0.0 copy-done
  29.0 0.0 copy-done.3
  29.0 0.0 copy-done.4
  29.0 0.0 copy-done.6
  29.0 0.0 copy-done.7
  29.0 0.0 copy-done.8
  29.0 0.0 copy-done.9
  29.0 2.8 %forces_first.1 = (bf16[512,128]{1,0:T(8,128)(2,1)S(1)}, bf16[192,512]{1,0:T(8,128)(2,1)S(1)}, bf16[512,256]{1,0:T(8,128)(2,1)S(1)}, f32[192,128]{1,0:T(8,128)S(...) custom-call(f32[64,128]{1,0:T(8,128)S(1)} %get-tuple-element.25.alive_ref, ...), custom_call_target="tpu_custom_call" | custom-call | tf_op jit(solution)/shard_map/forces_first/pallas_call | solution.py:29
  31.8 15.4 %all_to_all.46 = bf16[64,8,128]{2,1,0:T(8,128)(2,1)S(1)} all-to-all(bf16[64,8,128]{2,1,0:T(8,128)(2,1)S(1)} %bitcast.46), channel_id=1, replica_groups=mesh['z'=8,'x'=4,'c'=2,'solid'=8] {'z','x','c'}, dimensions={0} | all-to-all | bytes 262144 | tf_op jit(solution)/shard_map/all_to_all | solution.py:25
  47.2 0.7 owner_first.1
  47.9 14.4 %all_to_all.47.in_ref = f32[16,1,128]{2,1,0:T(1,128)S(1)} all-to-all(f32[16,1,128]{2,1,0:T(1,128)S(1)} %get-tuple-element.30), channel_id=1, replica_groups=mesh['z'=8,'x'=4,'c'=2,'solid'=8] {'c','solid'}, dimensions={0} | all-to-all | bytes 16384 | tf_op jit(solution)/shard_map/all_to_all | solution.py:25
  62.3 0.1 near_first.1
  62.4 11.7 %all_to_all.48.in_ref = f32[32,2,128]{2,1,0:T(2,128)S(1)} all-to-all(f32[32,2,128]{2,1,0:T(2,128)S(1)} %near_first.1), channel_id=1, replica_groups=mesh['z'=8,'x'=4,'c'=2,'solid'=8] {'z','x'}, dimensions={0} | all-to-all | bytes 65536 | tf_op jit(solution)/shard_map/all_to_all | solution.py:25
  74.0 3.0 %far_first.1 = (bf16[512,128]{1,0:T(8,128)(2,1)S(1)}, f32[12,128]{1,0:T(8,128)S(1)}, f32[56,128]{1,0:T(8,128)S(1)}) custom-call(f32[32,2,128]{2,1,0:T(2,128)S(1)} %all_to_all.48.in_ref, f32[12,128]{1,0:T(8,128)S(1)} %get-tuple-element.31.image_ref.last_ref, f32[600,128]{1,0:T(8,128)S(1)} %bitcast.38, bf16[512,128]{1,0:T(8,128)(2,1)S(1)} %get-tuple-element.32.qt_ref), custom_call_target="tpu_custom_call" | custom-call | tf_op jit(solution)/shard_map/far_first/pallas_call | solution.py:29
  77.0 16.7 %all_to_all.49 = bf16[64,8,128]{2,1,0:T(8,128)(2,1)S(1)} all-to-all(bf16[64,8,128]{2,1,0:T(8,128)(2,1)S(1)} %bitcast.48), channel_id=1, replica_groups=mesh['z'=8,'x'=4,'c'=2,'solid'=8] {'z','x','c'}, dimensions={0} | all-to-all | bytes 262144 | tf_op jit(solution)/shard_map/all_to_all | solution.py:25
  93.7 2.2 %forces_next.1 = bf16[512,128]{1,0:T(8,128)(2,1)S(1)} custom-call(bf16[512,128]{1,0:T(8,128)(2,1)S(1)} %bitcast.43, bf16[192,512]{1,0:T(8,128)(2,1)S(1)} %get-tuple-element.34.pick_ref, bf16[512,256]{1,0:T(8,128)(2,1)S(1)} %get-tuple-element.35.back_ref, bf16[64,128,128]{2,1,0:T(8,128)(2,1)S(1)} %copy-done, f32[192,128]{1,0:T(8,128)S(1)} %get-tuple-element.36.load_ref, ...), custom_call_target="tpu_custom_call" | custom-call | tf_op jit(solution)/shard_map/forces_next/pallas_call | solution.py:29
  95.9 14.9 %all_to_all.50 = bf16[64,8,128]{2,1,0:T(8,128)(2,1)S(1)} all-to-all(bf16[64,8,128]{2,1,0:T(8,128)(2,1)S(1)} %bitcast.44), channel_id=1, replica_groups=mesh['z'=8,'x'=4,'c'=2,'solid'=8] {'z','x','c'}, dimensions={0} | all-to-all | bytes 262144 | tf_op jit(solution)/shard_map/all_to_all | solution.py:25
  110.9 0.4 owner_next.1
  111.2 9.8 %all_to_all.51.in_ref = f32[16,1,128]{2,1,0:T(1,128)S(1)} all-to-all(f32[16,1,128]{2,1,0:T(1,128)S(1)} %get-tuple-element.41), channel_id=1, replica_groups=mesh['z'=8,'x'=4,'c'=2,'solid'=8] {'c','solid'}, dimensions={0} | all-to-all | bytes 16384 | tf_op jit(solution)/shard_map/all_to_all | solution.py:25
  121.1 11.6 %all_to_all.52.in_ref = f32[32,1,128]{2,1,0:T(1,128)S(1)} all-to-all(f32[32,1,128]{2,1,0:T(1,128)S(1)} %near_next.1), channel_id=1, replica_groups=mesh['z'=8,'x'=4,'c'=2,'solid'=8] {'z','x'}, dimensions={0} | all-to-all | bytes 32768 | tf_op jit(solution)/shard_map/all_to_all | solution.py:25
  132.7 3.1 %far_next.1 = (bf16[512,128]{1,0:T(8,128)(2,1)S(1)}, f32[12,128]{1,0:T(8,128)S(1)}) custom-call(f32[32,1,128]{2,1,0:T(1,128)S(1)} %all_to_all.52.in_ref, f32[56,128]{1,0:T(8,128)S(1)} %get-tuple-element.42.gram_ref, f32[12,128]{1,0:T(8,128)S(1)} %get-tuple-element.43.image_ref, f32[12,128]{1,0:T(8,128)S(1)} %get-tuple-element.31.image_ref.last_ref, ...), custom_call_target="tpu_custom_call" | custom-call | tf_op jit(solution)/shard_map/far_next/pallas_call | solution.py:29
  135.8 16.6 %all_to_all.53 = bf16[64,8,128]{2,1,0:T(8,128)(2,1)S(1)} all-to-all(bf16[64,8,128]{2,1,0:T(8,128)(2,1)S(1)} %bitcast.47), channel_id=1, replica_groups=mesh['z'=8,'x'=4,'c'=2,'solid'=8] {'z','x','c'}, dimensions={0} | all-to-all | bytes 262144 | tf_op jit(solution)/shard_map/all_to_all | solution.py:25
  152.3 1.5 final.1
  (7 shorter events, 0.0 us)
Async XLA Ops:
  1.3 0.7 copy-start.5
  2.0 27.0 %copy-start = (bf16[64,128,128]{2,1,0:T(8,128)(2,1)S(1)}, bf16[64,128,128]{2,1,0:T(8,128)(2,1)}, u32[]{:S(2)}) copy-start(bf16[64,128,128]{2,1,0:T(8,128)(2,1)} %map_ref.5) | copy-start | bytes 6291460
  2.0 27.0 %copy-start.1 = (f32[50,1,4,3,128]{4,2,3,1,0:T(4,128)S(1)}, f32[50,1,4,3,128]{4,2,3,1,0:T(4,128)}, u32[]{:S(2)}) copy-start(f32[50,1,4,3,128]{4,2,3,1,0:T(4,128)} %param.18) | copy-start | bytes 921604
  2.0 27.0 %copy-start.3 = (f32[64,3,128]{2,0,1:T(8,128)S(1)}, f32[64,3,128]{2,0,1:T(8,128)}, u32[]{:S(2)}) copy-start(f32[64,3,128]{2,0,1:T(8,128)} %param.10) | copy-start | bytes 294916
  2.0 27.0 %copy-start.4 = (f32[64,3,128]{2,0,1:T(8,128)S(1)}, f32[64,3,128]{2,0,1:T(8,128)}, u32[]{:S(2)}) copy-start(f32[64,3,128]{2,0,1:T(8,128)} %param.11) | copy-start | bytes 294916
  2.0 27.0 %copy-start.6 = (f32[1,4,3,128]{3,1,2,0:T(4,128)S(1)}, f32[1,4,3,128]{3,1,2,0:T(4,128)}, u32[]{:S(2)}) copy-start(f32[1,4,3,128]{3,1,2,0:T(4,128)} %param.17) | copy-start | bytes 18436
  2.0 27.0 %copy-start.7 = (f32[1,4,3,128]{3,1,2,0:T(4,128)S(1)}, f32[1,4,3,128]{3,1,2,0:T(4,128)}, u32[]{:S(2)}) copy-start(f32[1,4,3,128]{3,1,2,0:T(4,128)} %param.16) | copy-start | bytes 18436
  2.0 27.0 %copy-start.8 = (s32[64,1]{0,1:T(1,128)S(1)}, s32[64,1]{0,1:T(1,128)}, u32[]{:S(2)}) copy-start(s32[64,1]{0,1:T(1,128)} %param.14) | copy-start | bytes 772
  2.0 27.0 %copy-start.9 = (s32[64]{0:T(128)S(1)}, s32[64]{0:T(128)}, u32[]{:S(2)}) copy-start(s32[64]{0:T(128)} %param.15) | copy-start | bytes 772
  2.1 72.0 %copy-start.2 = (f32[50,1,4,3,128]{4,2,3,1,0:T(4,128)S(1)}, f32[50,1,4,3,128]{4,2,3,1,0:T(4,128)}, u32[]{:S(2)}) copy-start(f32[50,1,4,3,128]{4,2,3,1,0:T(4,128)} %param.19) | copy-start | bytes 921604

commit v4 on v3

--- a/solution.py
+++ b/solution.py
@@ -59,14 +59,20 @@
     return jnp.sum(jnp.where(on_diag, row, jnp.zeros_like(row)), axis=1, keepdims=True)
 
 
+def sixths(i):
+    peer = jnp.floor((i.astype(F32) + 0.5) * (1.0 / 6.0)).astype(jnp.int32)
+    row = i - 6 * peer
+    return peer, row // 2, row % 2
+
+
 def spread_kernel(live_ref, x_ref, out_ref, alive_ref):
+    out_ref[...] = jnp.broadcast_to(x_ref[...].astype(BF16)[None], out_ref.shape)
     alive_ref[...] = jnp.where(rows_of(alive_ref.shape) < live_ref[0], 1.0, 0.0)
-    out_ref[...] = jnp.broadcast_to(x_ref[...].astype(BF16)[None], out_ref.shape)
 
 
 def forces_first_kernel(
     alive_ref, x_ref, dest_ref, local_ref, hist_ref, raw_load_ref, raw_stiff_ref, map_ref, comp_ref, start_ref,
-    out_ref, pick_ref, back_ref, load_ref, stiff_ref, flat_comp_ref, flat_start_ref, gs, ss, whole_ref, xs, us,
+    out_ref, pick_ref, back_ref, load_ref, stiff_ref, flat_comp_ref, flat_start_ref, gs, ss, whole_ref, back_first_ref, xs, us,
 ):
     for c in range(3):
         flat_comp_ref[4 * c : 4 * c + 4, :] = comp_ref[c]
@@ -82,20 +88,21 @@
     slot_column = jnp.sum(jnp.where(same & (lanes < rows), 1.0, 0.0), axis=1, keepdims=True)
     slot_row = jnp.sum(jnp.where(same & (rows < lanes), 1.0, 0.0), axis=0, keepdims=True)
     slot_column = slot_column.astype(jnp.int32)
-    place_column = dest_column * 8 + slot_column * 4
     place_row = dest[0:1] * 8 + slot_row.astype(jnp.int32) * 4
-    wide = lanes_of((64, 512))
+    wide = lanes_of((64, 384))
     wider = lanes_of((64, 768))
     for c in range(3):
-        pick_ref[64 * c : 64 * c + 64, :] = jnp.where(wide == place_column + c, 1.0, 0.0).astype(BF16)
+        pick_ref[64 * c : 64 * c + 64, :] = jnp.where(wide == dest_column * 6 + 2 * c + slot_column, 1.0, 0.0).astype(BF16)
         whole_column = dest_column * PARTS + 4 * c + local_column
         whole_ref[64 * c : 64 * c + 64, :] = jnp.where(wider == whole_column, 1.0, 0.0).astype(BF16)
-    tall = rows_of((512, 128))
     low = lanes[0:1] < 64
-    first = jnp.where(low, place_row, pltpu.roll(place_row, 64, 1) + 1)
-    second = jnp.where(low, place_row + 2, -1)
-    back_ref[:, 0:128] = jnp.where(tall == first, 1.0, 0.0).astype(BF16)
-    back_ref[:, 128:256] = jnp.where(tall == second, 1.0, 0.0).astype(BF16)
+    place_next = dest[0:1] * 6 + slot_row.astype(jnp.int32)
+    for place, step, ref in ((place_row, 1, back_first_ref), (place_next, 2, back_ref)):
+        tall = rows_of((ref.shape[0], 128))
+        first = jnp.where(low, place, pltpu.roll(place, 64, 1) + step)
+        second = jnp.where(low, place + 2 * step, -1)
+        ref[:, 0:128] = jnp.where(tall == first, 1.0, 0.0).astype(BF16)
+        ref[:, 128:256] = jnp.where(tall == second, 1.0, 0.0).astype(BF16)
     part = lanes % 16
     held = (lanes >= 64) & (lanes // 16 - 4 == slot_column) & (part % 4 == local_column) & (part < PARTS)
     onto = jnp.where(dest == rows, 1.0, 0.0).astype(BF16)
@@ -114,7 +121,7 @@
     for c in range(3):
         load_ref[64 * c : 64 * c + 64, :] = raw_load_ref[64 * c : 64 * c + 64, :] * alive
         stiff_ref[64 * c : 64 * c + 64, :] = raw_stiff_ref[64 * c : 64 * c + 64, :] * alive
-    filled = forces(x_ref, whole_ref, back_ref, map_ref, load_ref, stiff_ref, xs, us)
+    filled = forces(x_ref, whole_ref, back_first_ref, map_ref, load_ref, stiff_ref, xs, us)
     out_ref[...] = (filled + ss[...]).astype(BF16)
 
 
@@ -138,8 +145,7 @@
 
 
 def final_kernel(x_ref, pick_ref, map_ref, alive_ref, struct_ref, out_ref, disp_ref, xs, us):
-    for c in range(3):
-        disp_ref[c] = struct_ref[4 * c : 4 * c + 4, :]
+    disp_ref[...] = struct_ref[...]
     xs[...] = dot(pick_ref[...], x_ref[...])
     apply_maps(map_ref, xs, us, ((1,), (0,)))
     for c in range(3):
@@ -176,11 +182,18 @@
     match = (part // 4 == row % 4) & (part < PARTS)
     q = jnp.where(match & (row < 4), wide[64:80], 0.0)
     q = (q + jnp.where(match & (row >= 4), wide[80:96], 0.0)).astype(BF16)
-    q_ref[...] = q
-    tall = jnp.broadcast_to(xs[...].reshape(64, 8, 128)[:, 7:8, :], (64, 8, 128)).reshape(512, 128)
-    lane = lanes_of((512, 128))
-    row = rows_of((512, 128)) % 8
-    match = ((lane % 16) // 4 == row % 4) & (lane // 16 - 4 == row // 4) & (lane % 16 < PARTS)
+    peer, component, place = sixths(lanes_of((64, 384)))
+    spread = jnp.where(peer == rows_of((64, 384)), 1.0, 0.0).astype(BF16)
+    wide = dot(mark7.astype(BF16), spread, ((0,), (0,)))
+    part = rows_of((16, 384))
+    match = (part // 4 == component[0:16]) & (part < PARTS)
+    later = jnp.where(match & (place[0:16] == 0), wide[64:80], 0.0)
+    q_ref[...] = (later + jnp.where(match & (place[0:16] == 1), wide[80:96], 0.0)).astype(BF16)
+    peer, component, place = sixths(rows_of((384, 128)))
+    lane = lanes_of((384, 128))
+    spread = jnp.where(peer == lane, 1.0, 0.0).astype(BF16)
+    tall = dot(spread[:, 0:64], mark7.astype(BF16))
+    match = ((lane % 16) // 4 == component) & (lane // 16 - 4 == place) & (lane % 16 < PARTS)
     qt_ref[...] = jnp.where(match, tall, 0.0).astype(BF16)
     image = comp_ref[...] * dot(q, got)[0:PARTS]
     resid = image - x_ref[...]
@@ -234,18 +247,27 @@
     a = jnp.where(lanes == WIDE, as_column(right * scale, gram.shape), a)
     tiles = [a[8 * i : 8 * i + 8] for i in range(COLS // 8)]
     sub = rows_of((8, 128))
+    column = lambda k: [jnp.broadcast_to(tile[:, k : k + 1], (8, 128)) for tile in tiles]
+    at = lambda stack, k: stack[k // 8][k % 8 : k % 8 + 1]
+    lefts, rights = column(0), column(1)
     for k in range(0, HIST, 2):
-        t, s = k // 8, k % 8
-        lefts = [jnp.broadcast_to(tile[:, k : k + 1], (8, 128)) for tile in tiles]
-        rights = [jnp.broadcast_to(tile[:, k + 1 : k + 2], (8, 128)) for tile in tiles]
-        p11, p12 = lefts[t][s : s + 1], rights[t][s : s + 1]
-        p21, p22 = lefts[t][s + 1 : s + 2], rights[t][s + 1 : s + 2]
-        row1, row2 = tiles[t][s : s + 1], tiles[t][s + 1 : s + 2]
+        coming = [(j, column(j)) for j in (k + 2, k + 3) if j < HIST]
+        p11, p12, p21, p22 = at(lefts, k), at(rights, k), at(lefts, k + 1), at(rights, k + 1)
         inverse = 1.0 / (p11 * p22 - p12 * p21)
-        new1 = (p22 * row1 - p12 * row2) * inverse
-        new2 = (p11 * row2 - p21 * row1) * inverse
-        tiles = [tile - left * new1 - right * new2 for tile, left, right in zip(tiles, lefts, rights)]
-        tiles[t] = jnp.where(sub == s, new1, jnp.where(sub == s + 1, new2, tiles[t]))
+
+        def scaled(one, two):
+            return (p22 * one - p12 * two) * inverse, (p11 * two - p21 * one) * inverse
+
+        def reduced(stack, new1, new2):
+            out = [v - left * new1 - right * new2 for v, left, right in zip(stack, lefts, rights)]
+            t, r = k // 8, k % 8
+            out[t] = jnp.where(sub == r, new1, jnp.where(sub == r + 1, new2, out[t]))
+            return out
+
+        following = [reduced(old, *scaled(at(lefts, j), at(rights, j))) for j, old in coming]
+        tiles = reduced(tiles, *scaled(at(tiles, k), at(tiles, k + 1)))
+        if following:
+            lefts, rights = following
     a = jnp.concatenate(tiles, axis=0)
     return -jnp.broadcast_to(a[:, WIDE : WIDE + 1], a.shape)[:HIST]
 
@@ -294,7 +316,8 @@
     step = image - last_ref[...]
     first = rows_of((HIST, 128)) == 0
     x = moved(image, coefficients, lambda m: jnp.where(first, step[m : m + 1, :], every(upd_ref, m)))
-    x_ref[...] = x
+    for c in range(3):
+        x_ref[c] = x[4 * c : 4 * c + 4, :]
     send_ref[...] = chosen(x, qt_ref[...], xs)
 
 
@@ -314,7 +337,8 @@
     peers = lax.axis_size(FLUID)
     near, far = lax.axis_size(NEAR), lax.axis_size(FAR)
     rows = 8 * peers
-    over_fluid = lambda x: exchange(x.reshape(peers, 8, 128), FLUID).reshape(rows, 128)
+    later = 6 * peers
+    over_fluid = lambda x: exchange(x.reshape(peers, 3, 2, 128), FLUID).reshape(later, 128)
     parts = lambda a: jnp.swapaxes(a, -3, -2)
     history, updates = (parts(a).reshape(-1, 128) for a in (residual_history, update_history))
     by_part = lambda a: jnp.swapaxes(a, 0, 1).reshape(3 * blocks, 128)
@@ -338,8 +362,8 @@
         "forces_first",
         [
             ((rows, 128), BF16),
-            ((3 * blocks, rows), BF16),
-            ((rows, 256), BF16),
+            ((3 * blocks, later), BF16),
+            ((later, 256), BF16),
             ((3 * blocks, 128), F32),
             ((3 * blocks, 128), F32),
             ((PARTS, 128), F32),
@@ -359,16 +383,17 @@
             pltpu.VMEM((64, 128), F32),
             tall,
             pltpu.VMEM((3 * blocks, PARTS * peers), BF16),
+            pltpu.VMEM((rows, 256), BF16),
             lines,
             lines,
         ],
         mib=8,
     )
-    got = over_fluid(sent)
+    got = exchange(sent.reshape(peers, 8, 128), FLUID).reshape(rows, 128)
     line, image, resid, q, qt = call(
         owner_first_kernel,
         "owner_first",
-        [((near, 1, 128), F32), ((PARTS, 128), F32), ((PARTS, 128), F32), ((16, rows), BF16), ((rows, 128), BF16)],
+        [((near, 1, 128), F32), ((PARTS, 128), F32), ((PARTS, 128), F32), ((16, later), BF16), ((later, 128), BF16)],
         got,
         comp,
         start,
@@ -382,7 +407,7 @@
     sent, x, gram = call(
         far_first_kernel,
         "far_first",
-        [((rows, 128), BF16), ((PARTS, 128), F32), ((COLS, 128), F32)],
+        [((later, 128), BF16), ((PARTS, 128), F32), ((COLS, 128), F32)],
         line,
         image,
         updates,
@@ -393,7 +418,7 @@
     sent = call(
         forces_next_kernel,
         "forces_next",
-        [((rows, 128), BF16)],
+        [((later, 128), BF16)],
         got,
         pick,
         back,
@@ -423,7 +448,7 @@
     sent, struct_disp = call(
         far_next_kernel,
         "far_next",
-        [((rows, 128), BF16), ((PARTS, 128), F32)],
+        [((later, 128), BF16), ((3, 4, 128), F32)],
         line,
         gram,
         image,

time: 154 us -> 150 us (0.974)
  Pallas kernels: 13.8 us -> 11.7 us
  blocking collectives: 138 us -> 136 us
    pallas_call x10, Pallas kernels: 13.8 us -> 11.7 us  [call(): pl.pallas_call(kernel, out_shape=[jax.ShapeDtypeStruct(shape, dtype) for...]
    all_to_all x9, blocking collectives: 138 us -> 136 us  [exchange(): return lax.all_to_all(x, axes, split_axis=0, concat_axis=0, tiled=True)]
where the time goes in v4:
time: 150 us
  blocking collectives  136 us (91%)
  Pallas kernels  11.7 us (8%)
    all_to_all x9, blocking collectives, exchange(): return lax.all_to_all(x, axes, split_axis=0, concat_axis=0, tiled=True)  136 us
    pallas_call x10, Pallas kernels, call(): pl.pallas_call(kernel, out_shape=[jax.ShapeDtypeStruct(shape, dtype) for...  11.7 us

profile of v4, /device:TPU:1, one launch (start us, length us, event | category | flops | bytes accessed | tf_op | source)
XLA Modules:
  0.0 149.7 jit_solution(659436016841517574)
XLA Ops:
  1.3 0.0 copy-start.5
  1.3 0.7 copy-done.5
  2.0 0.0 copy-start.6
  2.0 0.0 copy-start.7
  2.0 0.0 copy-start.8
  2.0 0.0 copy-start.9
  2.0 0.1 spread.1
  2.1 0.0 copy-start.2
  2.1 26.9 %all_to_all.45 = bf16[64,3,4,128]{3,2,1,0:T(4,128)(2,1)S(1)} all-to-all(bf16[64,3,4,128]{3,2,1,0:T(4,128)(2,1)S(1)} %get-tuple-element.26), channel_id=1, replica_groups=mesh['z'=8,'x'=4,'c'=2,'solid'=8] {'z','x','c'}, dimensions={0} | all-to-all | bytes 393216 | tf_op jit(solution)/shard_map/all_to_all | solution.py:25
  29.0 0.0 copy-done
  29.0 0.0 copy-done.1
  29.0 0.0 copy-done.3
  29.0 0.0 copy-done.4
  29.0 0.0 copy-done.6
  29.0 0.0 copy-done.7
  29.0 2.8 %forces_first.1 = (bf16[512,128]{1,0:T(8,128)(2,1)S(1)}, bf16[192,384]{1,0:T(8,128)(2,1)S(1)}, bf16[384,256]{1,0:T(8,128)(2,1)S(1)}, f32[192,128]{1,0:T(8,128)S(...) custom-call(f32[64,128]{1,0:T(8,128)S(1)} %get-tuple-element.25.alive_ref, ...), custom_call_target="tpu_custom_call" | custom-call | tf_op jit(solution)/shard_map/forces_first/pallas_call | solution.py:29
  31.8 15.4 %all_to_all.46 = bf16[64,8,128]{2,1,0:T(8,128)(2,1)S(1)} all-to-all(bf16[64,8,128]{2,1,0:T(8,128)(2,1)S(1)} %bitcast.46), channel_id=1, replica_groups=mesh['z'=8,'x'=4,'c'=2,'solid'=8] {'z','x','c'}, dimensions={0} | all-to-all | bytes 262144 | tf_op jit(solution)/shard_map/all_to_all | solution.py:25
  47.2 0.8 owner_first.1
  48.0 14.3 %all_to_all.47.in_ref = f32[16,1,128]{2,1,0:T(1,128)S(1)} all-to-all(f32[16,1,128]{2,1,0:T(1,128)S(1)} %get-tuple-element.30), channel_id=1, replica_groups=mesh['z'=8,'x'=4,'c'=2,'solid'=8] {'c','solid'}, dimensions={0} | all-to-all | bytes 16384 | tf_op jit(solution)/shard_map/all_to_all | solution.py:25
  62.3 0.1 near_first.1
  62.4 11.7 %all_to_all.48.in_ref = f32[32,2,128]{2,1,0:T(2,128)S(1)} all-to-all(f32[32,2,128]{2,1,0:T(2,128)S(1)} %near_first.1), channel_id=1, replica_groups=mesh['z'=8,'x'=4,'c'=2,'solid'=8] {'z','x'}, dimensions={0} | all-to-all | bytes 65536 | tf_op jit(solution)/shard_map/all_to_all | solution.py:25
  74.0 0.0 copy-done.2
  74.0 1.9 %far_first.1 = (bf16[384,128]{1,0:T(8,128)(2,1)S(1)}, f32[12,128]{1,0:T(8,128)S(1)}, f32[56,128]{1,0:T(8,128)S(1)}) custom-call(f32[32,2,128]{2,1,0:T(2,128)S(1)} %all_to_all.48.in_ref, f32[12,128]{1,0:T(8,128)S(1)} %get-tuple-element.31.image_ref.last_ref, f32[600,128]{1,0:T(8,128)S(1)} %bitcast.38, bf16[384,128]{1,0:T(8,128)(2,1)S(1)} %get-tuple-element.32.qt_ref), custom_call_target="tpu_custom_call" | custom-call | tf_op jit(solution)/shard_map/far_first/pallas_call | solution.py:29
  75.9 16.1 %all_to_all.49 = bf16[64,3,2,128]{3,2,1,0:T(2,128)(2,1)S(1)} all-to-all(bf16[64,3,2,128]{3,2,1,0:T(2,128)(2,1)S(1)} %bitcast.48), channel_id=1, replica_groups=mesh['z'=8,'x'=4,'c'=2,'solid'=8] {'z','x','c'}, dimensions={0} | all-to-all | bytes 196608 | tf_op jit(solution)/shard_map/all_to_all | solution.py:25
  92.0 2.2 %forces_next.1 = bf16[384,128]{1,0:T(8,128)(2,1)S(1)} custom-call(bf16[384,128]{1,0:T(8,128)(2,1)S(1)} %bitcast.43, bf16[192,384]{1,0:T(8,128)(2,1)S(1)} %get-tuple-element.34.pick_ref, bf16[384,256]{1,0:T(8,128)(2,1)S(1)} %get-tuple-element.35.back_ref, bf16[64,128,128]{2,1,0:T(8,128)(2,1)S(1)} %copy-done, f32[192,128]{1,0:T(8,128)S(1)} %get-tuple-element.36.load_ref, ...), custom_call_target="tpu_custom_call" | custom-call | tf_op jit(solution)/shard_map/forces_next/pallas_call | solution.py:29
  94.2 14.3 %all_to_all.50 = bf16[64,3,2,128]{3,2,1,0:T(2,128)(2,1)S(1)} all-to-all(bf16[64,3,2,128]{3,2,1,0:T(2,128)(2,1)S(1)} %bitcast.44), channel_id=1, replica_groups=mesh['z'=8,'x'=4,'c'=2,'solid'=8] {'z','x','c'}, dimensions={0} | all-to-all | bytes 196608 | tf_op jit(solution)/shard_map/all_to_all | solution.py:25
  108.5 0.4 owner_next.1
  108.9 9.8 %all_to_all.51.in_ref = f32[16,1,128]{2,1,0:T(1,128)S(1)} all-to-all(f32[16,1,128]{2,1,0:T(1,128)S(1)} %get-tuple-element.41), channel_id=1, replica_groups=mesh['z'=8,'x'=4,'c'=2,'solid'=8] {'c','solid'}, dimensions={0} | all-to-all | bytes 16384 | tf_op jit(solution)/shard_map/all_to_all | solution.py:25
  118.7 11.6 %all_to_all.52.in_ref = f32[32,1,128]{2,1,0:T(1,128)S(1)} all-to-all(f32[32,1,128]{2,1,0:T(1,128)S(1)} %near_next.1), channel_id=1, replica_groups=mesh['z'=8,'x'=4,'c'=2,'solid'=8] {'z','x'}, dimensions={0} | all-to-all | bytes 32768 | tf_op jit(solution)/shard_map/all_to_all | solution.py:25
  130.3 2.0 %far_next.1 = (bf16[384,128]{1,0:T(8,128)(2,1)S(1)}, f32[3,4,128]{2,1,0:T(4,128)S(1)}) custom-call(f32[32,1,128]{2,1,0:T(1,128)S(1)} %all_to_all.52.in_ref, f32[56,128]{1,0:T(8,128)S(1)} %get-tuple-element.42.gram_ref, f32[12,128]{1,0:T(8,128)S(1)} %get-tuple-element.43.image_ref, f32[12,128]{1,0:T(8,128)S(1)} %get-tuple-element.31.image_ref.last_ref, ...), custom_call_target="tpu_custom_call" | custom-call | tf_op jit(solution)/shard_map/far_next/pallas_call | solution.py:29
  132.3 15.9 %all_to_all.53 = bf16[64,3,2,128]{3,2,1,0:T(2,128)(2,1)S(1)} all-to-all(bf16[64,3,2,128]{3,2,1,0:T(2,128)(2,1)S(1)} %bitcast.47), channel_id=1, replica_groups=mesh['z'=8,'x'=4,'c'=2,'solid'=8] {'z','x','c'}, dimensions={0} | all-to-all | bytes 196608 | tf_op jit(solution)/shard_map/all_to_all | solution.py:25
  148.2 1.5 %final.1 = (f32[192,128]{1,0:T(8,128)}, f32[3,4,128]{2,1,0:T(4,128)}) custom-call(bf16[384,128]{1,0:T(8,128)(2,1)S(1)} %bitcast.42, bf16[192,384]{1,0:T(8,128)(2,1)S(1)} %get-tuple-element.34.pick_ref, bf16[64,128,128]{2,1,0:T(8,128)(2,1)S(1)} %copy-done, f32[64,128]{1,0:T(8,128)S(1)} %get-tuple-element.25.alive_ref, ...), custom_call_target="tpu_custom_call" | custom-call | tf_op jit(solution)/shard_map/final/pallas_call | solution.py:29
  (7 shorter events, 0.0 us)
Async XLA Ops:
  1.3 0.7 copy-start.5
  2.0 27.0 %copy-start = (bf16[64,128,128]{2,1,0:T(8,128)(2,1)S(1)}, bf16[64,128,128]{2,1,0:T(8,128)(2,1)}, u32[]{:S(2)}) copy-start(bf16[64,128,128]{2,1,0:T(8,128)(2,1)} %map_ref.5) | copy-start | bytes 6291460
  2.0 27.0 %copy-start.1 = (f32[50,1,4,3,128]{4,2,3,1,0:T(4,128)S(1)}, f32[50,1,4,3,128]{4,2,3,1,0:T(4,128)}, u32[]{:S(2)}) copy-start(f32[50,1,4,3,128]{4,2,3,1,0:T(4,128)} %param.18) | copy-start | bytes 921604
  2.0 27.0 %copy-start.3 = (f32[64,3,128]{2,0,1:T(8,128)S(1)}, f32[64,3,128]{2,0,1:T(8,128)}, u32[]{:S(2)}) copy-start(f32[64,3,128]{2,0,1:T(8,128)} %param.10) | copy-start | bytes 294916
  2.0 27.0 %copy-start.4 = (f32[64,3,128]{2,0,1:T(8,128)S(1)}, f32[64,3,128]{2,0,1:T(8,128)}, u32[]{:S(2)}) copy-start(f32[64,3,128]{2,0,1:T(8,128)} %param.11) | copy-start | bytes 294916
  2.0 27.0 %copy-start.6 = (f32[1,4,3,128]{3,1,2,0:T(4,128)S(1)}, f32[1,4,3,128]{3,1,2,0:T(4,128)}, u32[]{:S(2)}) copy-start(f32[1,4,3,128]{3,1,2,0:T(4,128)} %param.17) | copy-start | bytes 18436
  2.0 27.0 %copy-start.7 = (f32[1,4,3,128]{3,1,2,0:T(4,128)S(1)}, f32[1,4,3,128]{3,1,2,0:T(4,128)}, u32[]{:S(2)}) copy-start(f32[1,4,3,128]{3,1,2,0:T(4,128)} %param.16) | copy-start | bytes 18436
  2.0 27.0 %copy-start.8 = (s32[64,1]{0,1:T(1,128)S(1)}, s32[64,1]{0,1:T(1,128)}, u32[]{:S(2)}) copy-start(s32[64,1]{0,1:T(1,128)} %param.14) | copy-start | bytes 772
  2.0 27.0 %copy-start.9 = (s32[64]{0:T(128)S(1)}, s32[64]{0:T(128)}, u32[]{:S(2)}) copy-start(s32[64]{0:T(128)} %param.15) | copy-start | bytes 772
  2.1 72.0 %copy-start.2 = (f32[50,1,4,3,128]{4,2,3,1,0:T(4,128)S(1)}, f32[50,1,4,3,128]{4,2,3,1,0:T(4,128)}, u32[]{:S(2)}) copy-start(f32[50,1,4,3,128]{4,2,3,1,0:T(4,128)} %param.19) | copy-start | bytes 921604

commit v5 on v4

--- a/solution.py
+++ b/solution.py
@@ -126,9 +126,16 @@
 
 
 def apply_maps(map_ref, from_ref, to_ref, dims):
-    for b in range(map_ref.shape[0]):
-        rows = pl.ds(b, 3, stride=64)
-        to_ref[rows, :] = dot(from_ref[rows, :].astype(BF16), map_ref[b], dims)
+    for b in range(0, map_ref.shape[0], 2):
+        first, second = pl.ds(b, 3, stride=64), pl.ds(b + 1, 3, stride=64)
+        both = jnp.concatenate([from_ref[first, :], from_ref[second, :]], axis=0).astype(BF16)
+        if dims == ((1,), (0,)):
+            maps = jnp.concatenate([map_ref[b], map_ref[b + 1]], axis=1)
+        else:
+            maps = map_ref[b : b + 2].reshape(256, 128)
+        out = dot(both, maps, dims)
+        to_ref[first, :] = out[0:3, 0:128]
+        to_ref[second, :] = out[3:6, 128:256]
 
 
 def forces(x_ref, pick_ref, back_ref, map_ref, load_ref, stiff_ref, xs, us):
@@ -244,14 +251,15 @@
     trace = jnp.sum(jnp.sum(jnp.where(diag, gram, 0.0), axis=1, keepdims=True), axis=0, keepdims=True)
     scale = 1.0 / trace
     a = gram * scale + jnp.where(diag, RIDGE_SHARE / HIST, 0.0)
-    a = jnp.where(lanes == WIDE, as_column(right * scale, gram.shape), a)
-    tiles = [a[8 * i : 8 * i + 8] for i in range(COLS // 8)]
-    sub = rows_of((8, 128))
-    column = lambda k: [jnp.broadcast_to(tile[:, k : k + 1], (8, 128)) for tile in tiles]
-    at = lambda stack, k: stack[k // 8][k % 8 : k % 8 + 1]
-    lefts, rights = column(0), column(1)
+    a = jnp.where(lanes == rows + WIDE, 1.0, a)
+    under = jnp.where(lanes_of(right.shape) < WIDE, right * scale, 0.0)
+    tiles = [a[8 * i : 8 * i + 8] for i in range(COLS // 8)] + [jnp.broadcast_to(under, (8, 128))]
+    spread = lambda k, start: [jnp.broadcast_to(tile[:, k : k + 1], (8, 128)) for tile in tiles[start:]]
+    lefts, rights = spread(0, 0), spread(1, 0)
     for k in range(0, HIST, 2):
-        coming = [(j, column(j)) for j in (k + 2, k + 3) if j < HIST]
+        first = k // 8
+        at = lambda stack, j: stack[j // 8 - first][j % 8 : j % 8 + 1]
+        coming = [(j, spread(j, first)) for j in (k + 2, k + 3) if j < HIST]
         p11, p12, p21, p22 = at(lefts, k), at(rights, k), at(lefts, k + 1), at(rights, k + 1)
         inverse = 1.0 / (p11 * p22 - p12 * p21)
 
@@ -259,17 +267,14 @@
             return (p22 * one - p12 * two) * inverse, (p11 * two - p21 * one) * inverse
 
         def reduced(stack, new1, new2):
-            out = [v - left * new1 - right * new2 for v, left, right in zip(stack, lefts, rights)]
-            t, r = k // 8, k % 8
-            out[t] = jnp.where(sub == r, new1, jnp.where(sub == r + 1, new2, out[t]))
-            return out
+            return [v - left * new1 - right * new2 for v, left, right in zip(stack, lefts, rights)]
 
         following = [reduced(old, *scaled(at(lefts, j), at(rights, j))) for j, old in coming]
-        tiles = reduced(tiles, *scaled(at(tiles, k), at(tiles, k + 1)))
+        tiles[first:] = reduced(tiles[first:], *scaled(at(tiles[first:], k), at(tiles[first:], k + 1)))
         if following:
-            lefts, rights = following
-    a = jnp.concatenate(tiles, axis=0)
-    return -jnp.broadcast_to(a[:, WIDE : WIDE + 1], a.shape)[:HIST]
+            lefts, rights = (stack[(k + 2) // 8 - first :] for stack in following)
+    solution_row = pltpu.roll(tiles[-1], WIDE, 1)[0:1]
+    return jnp.broadcast_to(as_column(solution_row, gram.shape), gram.shape)[:HIST]
 
 
 def moved(image, coefficients, column):

time: 150 us -> 148 us (0.987)
  Pallas kernels: 11.7 us -> 9.57 us
    pallas_call x10, Pallas kernels: 11.7 us -> 9.57 us  [call(): pl.pallas_call(kernel, out_shape=[jax.ShapeDtypeStruct(shape, dtype) for...]
where the time goes in v5:
time: 148 us
  blocking collectives  136 us (92%)
  Pallas kernels  9.57 us (6%)
    all_to_all x9, blocking collectives, exchange(): return lax.all_to_all(x, axes, split_axis=0, concat_axis=0, tiled=True)  136 us
    pallas_call x10, Pallas kernels, call(): pl.pallas_call(kernel, out_shape=[jax.ShapeDtypeStruct(shape, dtype) for...  9.57 us

profile of v5, /device:TPU:1, one launch (start us, length us, event | category | flops | bytes accessed | tf_op | source)
XLA Modules:
  0.0 147.6 jit_solution(2906532817212191544)
XLA Ops:
  1.3 0.0 copy-start.5
  1.3 0.7 copy-done.5
  2.0 0.0 copy-start.6
  2.0 0.0 copy-start.7
  2.0 0.0 copy-start.8
  2.0 0.0 copy-start.9
  2.0 0.1 spread.1
  2.1 0.0 copy-start.2
  2.1 26.9 %all_to_all.45 = bf16[64,3,4,128]{3,2,1,0:T(4,128)(2,1)S(1)} all-to-all(bf16[64,3,4,128]{3,2,1,0:T(4,128)(2,1)S(1)} %get-tuple-element.26), channel_id=1, replica_groups=mesh['z'=8,'x'=4,'c'=2,'solid'=8] {'z','x','c'}, dimensions={0} | all-to-all | bytes 393216 | tf_op jit(solution)/shard_map/all_to_all | solution.py:25
  29.0 0.0 copy-done
  29.0 0.0 copy-done.1
  29.0 0.0 copy-done.3
  29.0 0.0 copy-done.4
  29.0 0.0 copy-done.6
  29.0 0.0 copy-done.7
  29.0 0.0 copy-done.8
  29.0 2.0 %forces_first.1 = (bf16[512,128]{1,0:T(8,128)(2,1)S(1)}, bf16[192,384]{1,0:T(8,128)(2,1)S(1)}, bf16[384,256]{1,0:T(8,128)(2,1)S(1)}, f32[192,128]{1,0:T(8,128)S(...) custom-call(f32[64,128]{1,0:T(8,128)S(1)} %get-tuple-element.25.alive_ref, ...), custom_call_target="tpu_custom_call" | custom-call | tf_op jit(solution)/shard_map/forces_first/pallas_call | solution.py:29
  31.0 15.4 %all_to_all.46 = bf16[64,8,128]{2,1,0:T(8,128)(2,1)S(1)} all-to-all(bf16[64,8,128]{2,1,0:T(8,128)(2,1)S(1)} %bitcast.46), channel_id=1, replica_groups=mesh['z'=8,'x'=4,'c'=2,'solid'=8] {'z','x','c'}, dimensions={0} | all-to-all | bytes 262144 | tf_op jit(solution)/shard_map/all_to_all | solution.py:25
  46.4 0.8 owner_first.1
  47.2 14.3 %all_to_all.47.in_ref = f32[16,1,128]{2,1,0:T(1,128)S(1)} all-to-all(f32[16,1,128]{2,1,0:T(1,128)S(1)} %get-tuple-element.30), channel_id=1, replica_groups=mesh['z'=8,'x'=4,'c'=2,'solid'=8] {'c','solid'}, dimensions={0} | all-to-all | bytes 16384 | tf_op jit(solution)/shard_map/all_to_all | solution.py:25
  61.5 0.1 near_first.1
  61.6 11.7 %all_to_all.48.in_ref = f32[32,2,128]{2,1,0:T(2,128)S(1)} all-to-all(f32[32,2,128]{2,1,0:T(2,128)S(1)} %near_first.1), channel_id=1, replica_groups=mesh['z'=8,'x'=4,'c'=2,'solid'=8] {'z','x'}, dimensions={0} | all-to-all | bytes 65536 | tf_op jit(solution)/shard_map/all_to_all | solution.py:25
  73.3 1.8 %far_first.1 = (bf16[384,128]{1,0:T(8,128)(2,1)S(1)}, f32[12,128]{1,0:T(8,128)S(1)}, f32[56,128]{1,0:T(8,128)S(1)}) custom-call(f32[32,2,128]{2,1,0:T(2,128)S(1)} %all_to_all.48.in_ref, f32[12,128]{1,0:T(8,128)S(1)} %get-tuple-element.31.image_ref.last_ref, f32[600,128]{1,0:T(8,128)S(1)} %bitcast.38, bf16[384,128]{1,0:T(8,128)(2,1)S(1)} %get-tuple-element.32.qt_ref), custom_call_target="tpu_custom_call" | custom-call | tf_op jit(solution)/shard_map/far_first/pallas_call | solution.py:29
  75.0 16.1 %all_to_all.49 = bf16[64,3,2,128]{3,2,1,0:T(2,128)(2,1)S(1)} all-to-all(bf16[64,3,2,128]{3,2,1,0:T(2,128)(2,1)S(1)} %bitcast.48), channel_id=1, replica_groups=mesh['z'=8,'x'=4,'c'=2,'solid'=8] {'z','x','c'}, dimensions={0} | all-to-all | bytes 196608 | tf_op jit(solution)/shard_map/all_to_all | solution.py:25
  91.1 1.4 forces_next.1
  92.5 14.3 %all_to_all.50 = bf16[64,3,2,128]{3,2,1,0:T(2,128)(2,1)S(1)} all-to-all(bf16[64,3,2,128]{3,2,1,0:T(2,128)(2,1)S(1)} %bitcast.44), channel_id=1, replica_groups=mesh['z'=8,'x'=4,'c'=2,'solid'=8] {'z','x','c'}, dimensions={0} | all-to-all | bytes 196608 | tf_op jit(solution)/shard_map/all_to_all | solution.py:25
  106.8 0.4 owner_next.1
  107.2 9.8 %all_to_all.51.in_ref = f32[16,1,128]{2,1,0:T(1,128)S(1)} all-to-all(f32[16,1,128]{2,1,0:T(1,128)S(1)} %get-tuple-element.41), channel_id=1, replica_groups=mesh['z'=8,'x'=4,'c'=2,'solid'=8] {'c','solid'}, dimensions={0} | all-to-all | bytes 16384 | tf_op jit(solution)/shard_map/all_to_all | solution.py:25
  117.0 11.6 %all_to_all.52.in_ref = f32[32,1,128]{2,1,0:T(1,128)S(1)} all-to-all(f32[32,1,128]{2,1,0:T(1,128)S(1)} %near_next.1), channel_id=1, replica_groups=mesh['z'=8,'x'=4,'c'=2,'solid'=8] {'z','x'}, dimensions={0} | all-to-all | bytes 32768 | tf_op jit(solution)/shard_map/all_to_all | solution.py:25
  128.6 1.8 %far_next.1 = (bf16[384,128]{1,0:T(8,128)(2,1)S(1)}, f32[3,4,128]{2,1,0:T(4,128)S(1)}) custom-call(f32[32,1,128]{2,1,0:T(1,128)S(1)} %all_to_all.52.in_ref, f32[56,128]{1,0:T(8,128)S(1)} %get-tuple-element.42.gram_ref, f32[12,128]{1,0:T(8,128)S(1)} %get-tuple-element.43.image_ref, f32[12,128]{1,0:T(8,128)S(1)} %get-tuple-element.31.image_ref.last_ref, ...), custom_call_target="tpu_custom_call" | custom-call | tf_op jit(solution)/shard_map/far_next/pallas_call | solution.py:29
  130.5 15.9 %all_to_all.53 = bf16[64,3,2,128]{3,2,1,0:T(2,128)(2,1)S(1)} all-to-all(bf16[64,3,2,128]{3,2,1,0:T(2,128)(2,1)S(1)} %bitcast.47), channel_id=1, replica_groups=mesh['z'=8,'x'=4,'c'=2,'solid'=8] {'z','x','c'}, dimensions={0} | all-to-all | bytes 196608 | tf_op jit(solution)/shard_map/all_to_all | solution.py:25
  146.3 1.3 final.1
  (7 shorter events, 0.0 us)
Async XLA Ops:
  1.3 0.7 copy-start.5
  2.0 27.0 %copy-start = (bf16[64,128,128]{2,1,0:T(8,128)(2,1)S(1)}, bf16[64,128,128]{2,1,0:T(8,128)(2,1)}, u32[]{:S(2)}) copy-start(bf16[64,128,128]{2,1,0:T(8,128)(2,1)} %map_ref.5) | copy-start | bytes 6291460
  2.0 27.0 %copy-start.1 = (f32[50,1,4,3,128]{4,2,3,1,0:T(4,128)S(1)}, f32[50,1,4,3,128]{4,2,3,1,0:T(4,128)}, u32[]{:S(2)}) copy-start(f32[50,1,4,3,128]{4,2,3,1,0:T(4,128)} %param.18) | copy-start | bytes 921604
  2.0 27.0 %copy-start.3 = (f32[64,3,128]{2,0,1:T(8,128)S(1)}, f32[64,3,128]{2,0,1:T(8,128)}, u32[]{:S(2)}) copy-start(f32[64,3,128]{2,0,1:T(8,128)} %param.10) | copy-start | bytes 294916
  2.0 27.0 %copy-start.4 = (f32[64,3,128]{2,0,1:T(8,128)S(1)}, f32[64,3,128]{2,0,1:T(8,128)}, u32[]{:S(2)}) copy-start(f32[64,3,128]{2,0,1:T(8,128)} %param.11) | copy-start | bytes 294916
  2.0 27.0 %copy-start.6 = (f32[1,4,3,128]{3,1,2,0:T(4,128)S(1)}, f32[1,4,3,128]{3,1,2,0:T(4,128)}, u32[]{:S(2)}) copy-start(f32[1,4,3,128]{3,1,2,0:T(4,128)} %param.17) | copy-start | bytes 18436
  2.0 27.0 %copy-start.7 = (f32[1,4,3,128]{3,1,2,0:T(4,128)S(1)}, f32[1,4,3,128]{3,1,2,0:T(4,128)}, u32[]{:S(2)}) copy-start(f32[1,4,3,128]{3,1,2,0:T(4,128)} %param.16) | copy-start | bytes 18436
  2.0 27.0 %copy-start.8 = (s32[64,1]{0,1:T(1,128)S(1)}, s32[64,1]{0,1:T(1,128)}, u32[]{:S(2)}) copy-start(s32[64,1]{0,1:T(1,128)} %param.14) | copy-start | bytes 772
  2.0 27.0 %copy-start.9 = (s32[64]{0:T(128)S(1)}, s32[64]{0:T(128)}, u32[]{:S(2)}) copy-start(s32[64]{0:T(128)} %param.15) | copy-start | bytes 772
  2.1 71.2 %copy-start.2 = (f32[50,1,4,3,128]{4,2,3,1,0:T(4,128)S(1)}, f32[50,1,4,3,128]{4,2,3,1,0:T(4,128)}, u32[]{:S(2)}) copy-start(f32[50,1,4,3,128]{4,2,3,1,0:T(4,128)} %param.19) | copy-start | bytes 921604

commit v6 on v5

--- a/solution.py
+++ b/solution.py
@@ -19,19 +19,20 @@
 HIGHEST = lax.Precision.HIGHEST
 VMEM = pl.BlockSpec(memory_space=pltpu.VMEM)
 SMEM = pl.BlockSpec(memory_space=pltpu.SMEM)
+HBM = pl.BlockSpec(memory_space=pl.ANY)
 
 
 def exchange(x, axes):
     return lax.all_to_all(x, axes, split_axis=0, concat_axis=0, tiled=True)
 
 
-def call(kernel, name, outs, *args, in_specs=None, scratch=(), mib=2, cost=None):
+def call(kernel, name, outs, *args, in_specs=None, out_specs=None, scratch=(), mib=2, cost=None):
     return pl.pallas_call(
         kernel,
         out_shape=[jax.ShapeDtypeStruct(shape, dtype) for shape, dtype in outs],
         compiler_params=pltpu.CompilerParams(vmem_limit_bytes=mib << 20),
         in_specs=in_specs or [VMEM] * len(args),
-        out_specs=[VMEM] * len(outs),
+        out_specs=out_specs or [VMEM] * len(outs),
         scratch_shapes=list(scratch),
         cost_estimate=cost,
         name=name,
@@ -125,8 +126,8 @@
     out_ref[...] = (filled + ss[...]).astype(BF16)
 
 
-def apply_maps(map_ref, from_ref, to_ref, dims):
-    for b in range(0, map_ref.shape[0], 2):
+def apply_maps(map_ref, from_ref, to_ref, dims, blocks=range(0, 64, 2)):
+    for b in blocks:
         first, second = pl.ds(b, 3, stride=64), pl.ds(b + 1, 3, stride=64)
         both = jnp.concatenate([from_ref[first, :], from_ref[second, :]], axis=0).astype(BF16)
         if dims == ((1,), (0,)):
@@ -151,12 +152,19 @@
     out_ref[...] = forces(x_ref, pick_ref, back_ref, map_ref, load_ref, stiff_ref, xs, us).astype(BF16)
 
 
-def final_kernel(x_ref, pick_ref, map_ref, alive_ref, struct_ref, out_ref, disp_ref, xs, us):
-    disp_ref[...] = struct_ref[...]
+def final_kernel(x_ref, pick_ref, map_ref, alive_ref, struct_ref, out_ref, disp_ref, xs, us, done, sems):
+    copies = [pltpu.make_async_copy(struct_ref, disp_ref, sems.at[6])]
+    copies[0].start()
     xs[...] = dot(pick_ref[...], x_ref[...])
-    apply_maps(map_ref, xs, us, ((1,), (0,)))
-    for c in range(3):
-        out_ref[64 * c : 64 * c + 64, :] = us[64 * c : 64 * c + 64, :] * alive_ref[...]
+    for half in range(2):
+        apply_maps(map_ref, xs, us, ((1,), (0,)), range(32 * half, 32 * half + 32, 2))
+        for c in range(3):
+            rows = pl.ds(64 * c + 32 * half, 32)
+            done[rows, :] = us[rows, :] * alive_ref[32 * half : 32 * half + 32, :]
+            copies.append(pltpu.make_async_copy(done.at[rows, :], out_ref.at[rows, :], sems.at[3 * half + c]))
+            copies[-1].start()
+    for copy in copies:
+        copy.wait()
 
 
 def history_sums(hist_ref, vector):
@@ -472,7 +480,8 @@
         mapping,
         alive,
         struct_disp,
-        scratch=[lines, lines],
+        out_specs=[HBM, HBM],
+        scratch=[lines, lines, lines, pltpu.SemaphoreType.DMA((7,))],
         mib=6,
     )
     struct_disp = parts(struct_disp[None])

time: 148 us -> 148 us (level)
  no operation moved by 1% of the time
where the time goes in v6:
time: 148 us
  blocking collectives  136 us (92%)
  Pallas kernels  9.6 us (6%)
    all_to_all x9, blocking collectives, exchange(): return lax.all_to_all(x, axes, split_axis=0, concat_axis=0, tiled=True)  136 us
    pallas_call x10, Pallas kernels, call(): pl.pallas_call(kernel, out_shape=[jax.ShapeDtypeStruct(shape, dtype) for...  9.6 us

profile of v6, /device:TPU:1, one launch (start us, length us, event | category | flops | bytes accessed | tf_op | source)
XLA Modules:
  0.0 147.6 jit_solution(855252024437378206)
XLA Ops:
  1.3 0.0 copy-start.5
  1.3 0.7 copy-done.5
  2.0 0.0 copy-start.6
  2.0 0.0 copy-start.7
  2.0 0.0 copy-start.8
  2.0 0.0 copy-start.9
  2.0 0.1 spread.1
  2.1 0.0 copy-start.2
  2.1 26.9 %all_to_all.45 = bf16[64,3,4,128]{3,2,1,0:T(4,128)(2,1)S(1)} all-to-all(bf16[64,3,4,128]{3,2,1,0:T(4,128)(2,1)S(1)} %get-tuple-element.26), channel_id=1, replica_groups=mesh['z'=8,'x'=4,'c'=2,'solid'=8] {'z','x','c'}, dimensions={0} | all-to-all | bytes 393216 | tf_op jit(solution)/shard_map/all_to_all | solution.py:26
  29.0 0.0 copy-done
  29.0 0.0 copy-done.1
  29.0 0.0 copy-done.3
  29.0 0.0 copy-done.4
  29.0 0.0 copy-done.6
  29.0 0.0 copy-done.7
  29.0 0.0 copy-done.8
  29.0 2.0 %forces_first.1 = (bf16[512,128]{1,0:T(8,128)(2,1)S(1)}, bf16[192,384]{1,0:T(8,128)(2,1)S(1)}, bf16[384,256]{1,0:T(8,128)(2,1)S(1)}, f32[192,128]{1,0:T(8,128)S(...) custom-call(f32[64,128]{1,0:T(8,128)S(1)} %get-tuple-element.25.alive_ref, ...), custom_call_target="tpu_custom_call" | custom-call | tf_op jit(solution)/shard_map/forces_first/pallas_call | solution.py:30
  31.0 15.4 %all_to_all.46 = bf16[64,8,128]{2,1,0:T(8,128)(2,1)S(1)} all-to-all(bf16[64,8,128]{2,1,0:T(8,128)(2,1)S(1)} %bitcast.46), channel_id=1, replica_groups=mesh['z'=8,'x'=4,'c'=2,'solid'=8] {'z','x','c'}, dimensions={0} | all-to-all | bytes 262144 | tf_op jit(solution)/shard_map/all_to_all | solution.py:26
  46.4 0.8 owner_first.1
  47.2 14.3 %all_to_all.47.in_ref = f32[16,1,128]{2,1,0:T(1,128)S(1)} all-to-all(f32[16,1,128]{2,1,0:T(1,128)S(1)} %get-tuple-element.30), channel_id=1, replica_groups=mesh['z'=8,'x'=4,'c'=2,'solid'=8] {'c','solid'}, dimensions={0} | all-to-all | bytes 16384 | tf_op jit(solution)/shard_map/all_to_all | solution.py:26
  61.5 0.1 near_first.1
  61.6 11.7 %all_to_all.48.in_ref = f32[32,2,128]{2,1,0:T(2,128)S(1)} all-to-all(f32[32,2,128]{2,1,0:T(2,128)S(1)} %near_first.1), channel_id=1, replica_groups=mesh['z'=8,'x'=4,'c'=2,'solid'=8] {'z','x'}, dimensions={0} | all-to-all | bytes 65536 | tf_op jit(solution)/shard_map/all_to_all | solution.py:26
  73.3 1.8 %far_first.1 = (bf16[384,128]{1,0:T(8,128)(2,1)S(1)}, f32[12,128]{1,0:T(8,128)S(1)}, f32[56,128]{1,0:T(8,128)S(1)}) custom-call(f32[32,2,128]{2,1,0:T(2,128)S(1)} %all_to_all.48.in_ref, f32[12,128]{1,0:T(8,128)S(1)} %get-tuple-element.31.image_ref.last_ref, f32[600,128]{1,0:T(8,128)S(1)} %bitcast.38, bf16[384,128]{1,0:T(8,128)(2,1)S(1)} %get-tuple-element.32.qt_ref), custom_call_target="tpu_custom_call" | custom-call | tf_op jit(solution)/shard_map/far_first/pallas_call | solution.py:30
  75.0 16.1 %all_to_all.49 = bf16[64,3,2,128]{3,2,1,0:T(2,128)(2,1)S(1)} all-to-all(bf16[64,3,2,128]{3,2,1,0:T(2,128)(2,1)S(1)} %bitcast.48), channel_id=1, replica_groups=mesh['z'=8,'x'=4,'c'=2,'solid'=8] {'z','x','c'}, dimensions={0} | all-to-all | bytes 196608 | tf_op jit(solution)/shard_map/all_to_all | solution.py:26
  91.1 1.4 forces_next.1
  92.5 14.3 %all_to_all.50 = bf16[64,3,2,128]{3,2,1,0:T(2,128)(2,1)S(1)} all-to-all(bf16[64,3,2,128]{3,2,1,0:T(2,128)(2,1)S(1)} %bitcast.44), channel_id=1, replica_groups=mesh['z'=8,'x'=4,'c'=2,'solid'=8] {'z','x','c'}, dimensions={0} | all-to-all | bytes 196608 | tf_op jit(solution)/shard_map/all_to_all | solution.py:26
  106.8 0.4 owner_next.1
  107.2 9.8 %all_to_all.51.in_ref = f32[16,1,128]{2,1,0:T(1,128)S(1)} all-to-all(f32[16,1,128]{2,1,0:T(1,128)S(1)} %get-tuple-element.41), channel_id=1, replica_groups=mesh['z'=8,'x'=4,'c'=2,'solid'=8] {'c','solid'}, dimensions={0} | all-to-all | bytes 16384 | tf_op jit(solution)/shard_map/all_to_all | solution.py:26
  117.0 11.6 %all_to_all.52.in_ref = f32[32,1,128]{2,1,0:T(1,128)S(1)} all-to-all(f32[32,1,128]{2,1,0:T(1,128)S(1)} %near_next.1), channel_id=1, replica_groups=mesh['z'=8,'x'=4,'c'=2,'solid'=8] {'z','x'}, dimensions={0} | all-to-all | bytes 32768 | tf_op jit(solution)/shard_map/all_to_all | solution.py:26
  128.6 1.8 %far_next.1 = (bf16[384,128]{1,0:T(8,128)(2,1)S(1)}, f32[3,4,128]{2,1,0:T(4,128)S(1)}) custom-call(f32[32,1,128]{2,1,0:T(1,128)S(1)} %all_to_all.52.in_ref, f32[56,128]{1,0:T(8,128)S(1)} %get-tuple-element.42.gram_ref, f32[12,128]{1,0:T(8,128)S(1)} %get-tuple-element.43.image_ref, f32[12,128]{1,0:T(8,128)S(1)} %get-tuple-element.31.image_ref.last_ref, ...), custom_call_target="tpu_custom_call" | custom-call | tf_op jit(solution)/shard_map/far_next/pallas_call | solution.py:30
  130.5 15.9 %all_to_all.53 = bf16[64,3,2,128]{3,2,1,0:T(2,128)(2,1)S(1)} all-to-all(bf16[64,3,2,128]{3,2,1,0:T(2,128)(2,1)S(1)} %bitcast.47), channel_id=1, replica_groups=mesh['z'=8,'x'=4,'c'=2,'solid'=8] {'z','x','c'}, dimensions={0} | all-to-all | bytes 196608 | tf_op jit(solution)/shard_map/all_to_all | solution.py:26
  146.3 1.3 final.1
  (7 shorter events, 0.0 us)
Async XLA Ops:
  1.3 0.7 copy-start.5
  2.0 27.0 %copy-start = (bf16[64,128,128]{2,1,0:T(8,128)(2,1)S(1)}, bf16[64,128,128]{2,1,0:T(8,128)(2,1)}, u32[]{:S(2)}) copy-start(bf16[64,128,128]{2,1,0:T(8,128)(2,1)} %map_ref.5) | copy-start | bytes 6291460
  2.0 27.0 %copy-start.1 = (f32[50,1,4,3,128]{4,2,3,1,0:T(4,128)S(1)}, f32[50,1,4,3,128]{4,2,3,1,0:T(4,128)}, u32[]{:S(2)}) copy-start(f32[50,1,4,3,128]{4,2,3,1,0:T(4,128)} %param.18) | copy-start | bytes 921604
  2.0 27.0 %copy-start.3 = (f32[64,3,128]{2,0,1:T(8,128)S(1)}, f32[64,3,128]{2,0,1:T(8,128)}, u32[]{:S(2)}) copy-start(f32[64,3,128]{2,0,1:T(8,128)} %param.10) | copy-start | bytes 294916
  2.0 27.0 %copy-start.4 = (f32[64,3,128]{2,0,1:T(8,128)S(1)}, f32[64,3,128]{2,0,1:T(8,128)}, u32[]{:S(2)}) copy-start(f32[64,3,128]{2,0,1:T(8,128)} %param.11) | copy-start | bytes 294916
  2.0 27.0 %copy-start.6 = (f32[1,4,3,128]{3,1,2,0:T(4,128)S(1)}, f32[1,4,3,128]{3,1,2,0:T(4,128)}, u32[]{:S(2)}) copy-start(f32[1,4,3,128]{3,1,2,0:T(4,128)} %param.17) | copy-start | bytes 18436
  2.0 27.0 %copy-start.7 = (f32[1,4,3,128]{3,1,2,0:T(4,128)S(1)}, f32[1,4,3,128]{3,1,2,0:T(4,128)}, u32[]{:S(2)}) copy-start(f32[1,4,3,128]{3,1,2,0:T(4,128)} %param.16) | copy-start | bytes 18436
  2.0 27.0 %copy-start.8 = (s32[64,1]{0,1:T(1,128)S(1)}, s32[64,1]{0,1:T(1,128)}, u32[]{:S(2)}) copy-start(s32[64,1]{0,1:T(1,128)} %param.14) | copy-start | bytes 772
  2.0 27.0 %copy-start.9 = (s32[64]{0:T(128)S(1)}, s32[64]{0:T(128)}, u32[]{:S(2)}) copy-start(s32[64]{0:T(128)} %param.15) | copy-start | bytes 772
  2.1 71.2 %copy-start.2 = (f32[50,1,4,3,128]{4,2,3,1,0:T(4,128)S(1)}, f32[50,1,4,3,128]{4,2,3,1,0:T(4,128)}, u32[]{:S(2)}) copy-start(f32[50,1,4,3,128]{4,2,3,1,0:T(4,128)} %param.19) | copy-start | bytes 921604
